TPU v7x, 32 devices: a whole 2x2x4 slice. The times are simulated.
32 devices in a mesh: slab: 8 (over z, y), sub: 4 (over x, core).
Axes of the slice: x: 2, y: 2, z: 4, core: 2. Of those that a mesh axis runs over, the one named last changes fastest.
Arguments:
- coefficients: bfloat16 [7, 6, 6, 64, 12, 128], P(None, None, None, 'slab', 'sub'), may hold values from -1 to 1
- earlier: float32 [30, 6, 64, 12, 128], P(None, None, 'slab', 'sub'), may hold values from -6 to 6
- start: float32 [6, 64, 12, 128], P(None, 'slab', 'sub'), may hold values from -8 to 8
- shifts: float32 [5], replicated, may hold values from -0.3 to 0.3
Outputs:
- new_basis: float32 [6, 6, 64, 12, 128], P(None, None, 'slab', 'sub')
- projection: float32 [30, 6], replicated
- triangle: float32 [6, 6], replicated
All inputs are finite; a program needn't handle non-finite values.
Results may differ from a plain program's by a relative error of at most 0.0015.
Values may be sent and summed in bfloat16 or wider, within the bound.
A program may use at most 64 MiB of HBM per device.

v0:
```python
import functools

import jax
import jax.numpy as jnp
from jax import lax
from jax.experimental import pallas as pl
from jax.experimental.pallas import tpu as pltpu
from jax.sharding import PartitionSpec as P

MESH = pl.DeviceIdType.MESH
LANES = 128
ROWS = 8


def dot(a, b, nt=False):
    return lax.dot_general(
        a, b, (((1,), (1 if nt else 0,)), ((), ())),
        precision=lax.Precision.HIGHEST, preferred_element_type=jnp.float32,
    )


def iota(shape, dim):
    return lax.broadcasted_iota(jnp.int32, shape, dim)


def onehot(shape, test):
    return jnp.where(test(iota(shape, 0), iota(shape, 1)), 1.0, 0.0).astype(jnp.float32)


def factors(count):
    found = []
    while count > 1:
        size = max(f for f in range(2, min(count, 8) + 1) if count % f == 0) if any(
            count % f == 0 for f in range(2, min(count, 8) + 1)
        ) else count
        found.append(size)
        count //= size
    return found


def stages_of(sizes):
    found = []
    for axis, count in sizes:
        stride = 1
        for size in factors(count):
            found.append((axis, stride, size))
            stride *= size
    return found


def diagonal(value):
    r, q = iota(value.shape, 0), iota(value.shape, 1)
    return jnp.where((r & 7) == (q & 7), value, 0.0)


def split(value):
    first = value.astype(jnp.bfloat16)
    left = value - first.astype(jnp.float32)
    second = left.astype(jnp.bfloat16)
    third = (left - second.astype(jnp.float32)).astype(jnp.bfloat16)
    return [first, second, third]


def dot_pieces(a, b, nt=False):
    found = None
    rows = a[0].shape[0]
    for at in (2, 1, 0):
        left = jnp.concatenate(a[: 3 - at], axis=0)
        part = lax.dot_general(
            left, b[at], (((1,), (1 if nt else 0,)), ((), ())),
            preferred_element_type=jnp.float32,
        )
        for i in reversed(range(3 - at)):
            piece = part[i * rows:(i + 1) * rows]
            found = piece if found is None else found + piece
    return found


def side_by_side(value):
    count, width = value.shape[0], value.shape[1]
    return jnp.concatenate(
        [value[:, x].reshape(count * ROWS, LANES) for x in range(width)], axis=1
    )


def kernel(
    sizes, coef_hbm, early_hbm, start_hbm, shifts_ref, new_ref, small_ref,
    coef_in, coef, edge_coef, allv, pieces, acc_ref, halo_x, halo_z, send_z, ee, sums_ref,
    lines, mine, gathered, mine_ee, gathered_ee,
    in_sem, halo_send, halo_recv, red_send, red_recv,
):
    depth = shifts_ref.shape[0]
    earlier, comp, width = early_hbm.shape[:3]
    block = depth + 1
    count = comp * width * ROWS * LANES * sizes[0][1] * sizes[1][1]
    stages = stages_of(sizes)
    place = {axis: lax.axis_index(axis) for axis, _ in sizes}
    slab, sub = sizes[0], sizes[1]

    def peer(stage, offset):
        axis, stride, size = stage
        digit = lax.rem(place[axis] // stride, size)
        other = lax.rem(digit + offset, size)
        return axis, digit, other, place[axis] + (other - digit) * stride

    copy_start = pltpu.make_async_copy(start_hbm, allv.at[earlier], in_sem.at[0])
    copy_coef = pltpu.make_async_copy(coef_hbm, coef_in, in_sem.at[1])
    copy_early = pltpu.make_async_copy(early_hbm, allv.at[pl.ds(0, earlier)], in_sem.at[2])
    copy_start.start()
    copy_coef.start()
    copy_early.start()

    halo_x[...] = jnp.zeros_like(halo_x)
    halo_z[...] = jnp.zeros_like(halo_z)
    send_z[...] = jnp.zeros_like(send_z)
    ee[...] = jnp.zeros_like(ee)
    lines[...] = jnp.zeros_like(lines)
    sums_ref[...] = jnp.zeros_like(sums_ref)
    for k in range(1, block):
        allv[earlier + k] = jnp.zeros_like(allv[earlier + k])

    barrier = pltpu.get_barrier_semaphore()
    expected = 0
    for stage in stages:
        for offset in range(1, stage[2]):
            axis, _, _, target = peer(stage, offset)
            pl.semaphore_signal(barrier, inc=1, device_id={axis: target}, device_id_type=MESH)
            expected += 1
    extra = [(axis, n) for axis, n in sizes if len(factors(n)) > 1]
    for axis, n in extra:
        for off in (-1, 1):
            there = jnp.logical_and(place[axis] + off >= 0, place[axis] + off < n)

            @pl.when(there)
            def _():
                pl.semaphore_signal(
                    barrier, inc=1, device_id={axis: place[axis] + off}, device_id_type=MESH
                )

    def halo_copy(step, kind, side):
        axis, n = (slab, sub)[kind]
        if kind == 0:
            src, dst = send_z.at[step, side], halo_z.at[step, side]
        else:
            src = allv.at[earlier + step, :, width - 1 if side == 0 else 0]
            dst = halo_x.at[step, side]
        target = place[axis] + (1 if side == 0 else -1)
        return pltpu.make_async_remote_copy(
            src_ref=src, dst_ref=dst,
            send_sem=halo_send.at[step, kind, side], recv_sem=halo_recv.at[step, kind, side],
            device_id={axis: target}, device_id_type=MESH,
        )

    def has(kind, side, sending):
        axis, n = (slab, sub)[kind]
        upward = (side == 0) == sending
        return place[axis] < n - 1 if upward else place[axis] > 0

    def pack(step):
        for e in range(comp):
            for x in range(width):
                row = 4 * e + x
                tile = allv.at[earlier + step, e, x]
                send_z[step, 0, row:row + 1, :] = tile[ROWS - 1:ROWS, :]
                send_z[step, 1, row:row + 1, :] = tile[0:1, :]

    def send(step):
        for kind in (0, 1):
            for side in (0, 1):
                @pl.when(has(kind, side, True))
                def _():
                    halo_copy(step, kind, side).start()

    copy_start.wait()
    pack(0)
    for axis, n in extra:
        for off in (-1, 1):
            there = jnp.logical_and(place[axis] + off >= 0, place[axis] + off < n)

            @pl.when(there)
            def _():
                pl.semaphore_wait(barrier, 1)
    pl.semaphore_wait(barrier, expected)
    send(0)

    copy_coef.wait()

    @pl.loop(0, comp)
    def _(c):
        for d in range(coef.shape[0]):
            coef[d, c] = coef_in[d, c].astype(jnp.float32)
        edge_coef[c] = jnp.zeros_like(edge_coef[c])
        for e in range(comp):
            for x in range(width):
                edge_coef[c, e, x:x + 1, :] = coef[1, c, e, x, 0:1, :]
                edge_coef[c, e, 4 + x:5 + x, :] = coef[2, c, e, x, ROWS - 1:ROWS, :]

    copy_early.wait()

    def self_products(c):
        parts = split(side_by_side(allv[pl.ds(0, earlier), c]))
        for at, part in enumerate(parts):
            pieces[at, c] = part
        ee[...] += dot_pieces(parts, [parts[0], parts[1], parts[2]], nt=True)

    def cross_products(k):
        total, group = earlier + block, 6
        w = allv[earlier + k]
        for low in range(0, total, group):
            high = min(low + group, total)
            part = jnp.sum(w[None] * allv[low:high], axis=(1, 2))
            sums_ref[low:high, :] = jnp.sum(part, axis=1)
        line = dot(jnp.ones((ROWS, LANES), jnp.float32), sums_ref[...], nt=True)
        lines[pl.ds(k, 1), :] = line[0:1]

    def self_finish():
        span = earlier * ROWS
        wide = dot(diagonal(ee[...]), onehot((span, LANES), lambda r, q: (r >> 3) == (q & 31)))
        wide = jnp.where((iota(wide.shape, 0) >> 6) == (iota(wide.shape, 1) >> 5), wide, 0.0)
        mine_ee[0] = dot(onehot((ROWS, span), lambda r, q: ((q >> 3) & 7) == r), wide)

    def move(kind, at, offset, sending):
        axis, digit, other, target = peer(stages[at], offset)
        own, slots = (mine, gathered) if kind == 0 else (mine_ee, gathered_ee)
        return pltpu.make_async_remote_copy(
            src_ref=own.at[at], dst_ref=slots.at[at, digit],
            send_sem=red_send.at[kind, at, other],
            recv_sem=red_recv.at[kind, at, digit if sending else other],
            device_id={axis: target}, device_id_type=MESH,
        )

    def begin(kind, at):
        for offset in range(1, stages[at][2]):
            move(kind, at, offset, True).start()

    def finish(kind, at):
        own, slots = (mine, gathered) if kind == 0 else (mine_ee, gathered_ee)
        slots[at, peer(stages[at], 0)[1]] = own[at]
        for offset in range(1, stages[at][2]):
            move(kind, at, offset, False).wait_recv()
        whole = slots[at, 0]
        for other in range(1, stages[at][2]):
            whole = whole + slots[at, other]
        own[at + 1] = whole

    row3 = iota((width, ROWS, LANES), 1)
    lane3 = iota((width, ROWS, LANES), 2)
    row2 = iota((ROWS, LANES), 0)
    zero_tile = jnp.zeros((1, ROWS, LANES), jnp.float32)

    @pl.loop(0, depth)
    def _(step):
        acc = (1.0 - shifts_ref[step]) * allv[earlier + step]
        for e in range(comp):
            v = allv[earlier + step, e]
            near = [
                v,
                jnp.where(row3 > 0, pltpu.roll(v, 1, 1), 0.0),
                jnp.where(row3 < ROWS - 1, pltpu.roll(v, ROWS - 1, 1), 0.0),
                jnp.concatenate([zero_tile, v[:-1]], axis=0),
                jnp.concatenate([v[1:], zero_tile], axis=0),
                jnp.where(lane3 > 0, pltpu.roll(v, 1, 2), 0.0),
                jnp.where(lane3 < LANES - 1, pltpu.roll(v, LANES - 1, 2), 0.0),
            ]
            for d in range(len(near)):
                acc = acc + coef[d, :, e] * near[d][None]
        acc_ref[...] = acc

        cross_products(step)

        @pl.loop(
            jnp.minimum(step * comp // (depth - 2), comp),
            jnp.minimum((step + 1) * comp // (depth - 2), comp),
        )
        def _(c):
            self_products(c)

        @pl.when(step == depth - 2)
        def _():
            self_finish()
            begin(1, 0)

        @pl.when(step == depth - 1)
        def _():
            finish(1, 0)
            if len(stages) > 1:
                begin(1, 1)

        def arrive(kind):
            for side in (0, 1):
                @pl.when(has(kind, side, False))
                def _():
                    halo_copy(step, kind, side).wait_recv()

        arrive(1)
        low = acc_ref[:, 0]
        for e in range(comp):
            low = low + coef[3, :, e, 0] * halo_x[step, 0, e][None]
        acc_ref[:, 0] = low
        high = acc_ref[:, width - 1]
        for e in range(comp):
            high = high + coef[4, :, e, width - 1] * halo_x[step, 1, e][None]
        acc_ref[:, width - 1] = high

        arrive(0)
        edge = jnp.zeros((comp, ROWS, LANES), jnp.float32)
        for e in range(comp):
            base = ROWS * (e // 2)
            below = halo_z[step, 0, base:base + ROWS, :]
            above = halo_z[step, 1, base:base + ROWS, :]
            if e % 2 == 0:
                above = pltpu.roll(above, 4, 0)
            else:
                below = pltpu.roll(below, 4, 0)
            edge = edge + edge_coef[:, e] * jnp.where(row2 < 4, below, above)[None]
        for c in range(comp):
            for x in range(width):
                value = acc_ref[c, x]
                value = value + jnp.where(
                    row2 == 0, edge[c, x:x + 1, :],
                    jnp.where(row2 == ROWS - 1, edge[c, 4 + x:5 + x, :], 0.0),
                )
                allv[earlier + step + 1, c, x] = value

        @pl.when(step < depth - 1)
        def _():
            pack(step + 1)
            send(step + 1)

    cross_products(depth)
    total = earlier + block

    for r in range(ROWS // 2):
        odd = pltpu.roll(lines[2 * r + 1:2 * r + 2, :], LANES // 2, 1)
        mine[0, r:r + 1, :] = lines[2 * r:2 * r + 1, :] + odd
    for at in range(len(stages)):
        begin(0, at)
        if at + 1 < len(stages):
            finish(1, at + 1)
            if at + 2 < len(stages):
                begin(1, at + 2)
        finish(0, at)
    packed = mine_ee[len(stages)] * (1.0 / count)
    even = mine[len(stages)] * (1.0 / count)
    odd = pltpu.roll(even, LANES // 2, 1)
    found = jnp.concatenate(
        [(odd if k % 2 else even)[k // 2:k // 2 + 1] for k in range(ROWS)], axis=0
    )

    row, lane = iota((ROWS, LANES), 0), iota((ROWS, LANES), 1)
    proj_t = jnp.where(lane < earlier, found, 0.0)
    known = jnp.where(lane < earlier + row, found, 0.0)
    pick = onehot((ROWS, LANES), lambda r, q: q == r + earlier)
    gram = jnp.where(lane <= earlier + row, found, 0.0)
    gram = pltpu.roll(gram, LANES - earlier, 1)[:, :ROWS]
    square = jnp.concatenate(
        [packed] + [pltpu.roll(packed, LANES - 32 * g, 1) for g in range(1, 4)], axis=0
    )
    sr, sl = iota(square.shape, 0), iota(square.shape, 1)
    square = jnp.where(sl < 32, square, 0.0) - jnp.where(sr == sl, 2.0, 0.0)
    gram = gram + dot(dot(proj_t[:, :32], square) + pick, known, nt=True)

    upper = gram
    inverse = onehot((ROWS, ROWS), lambda r, q: r == q)
    r8 = iota((ROWS, ROWS), 0)
    q8 = iota((ROWS, ROWS), 1)
    for p in range(block):
        pivot = upper[p:p + 1, p:p + 1]
        scale = lax.rsqrt(pivot)
        scale = scale * (1.5 - 0.5 * pivot * scale * scale)
        column = upper[:, p:p + 1] * scale
        row_u, row_i = upper[p:p + 1, :] * scale, inverse[p:p + 1, :] * scale
        upper = jnp.where(r8 == p, row_u, jnp.where(r8 > p, upper - column * row_u, upper))
        inverse = jnp.where(r8 == p, row_i, jnp.where(r8 > p, inverse - column * row_i, inverse))
    small_ref[0:ROWS, :] = proj_t
    small_ref[ROWS:2 * ROWS, 0:ROWS] = jnp.where(q8 >= r8, upper, 0.0)

    mix = dot(inverse, pick - proj_t)
    tall = dot(onehot((block * ROWS, ROWS), lambda r, q: (r >> 3) == q), mix)
    span = earlier * ROWS
    mix = split(diagonal(dot(tall, onehot((LANES, span), lambda r, q: (q >> 3) == r))))
    weights = [
        [
            jnp.broadcast_to(
                tall[k * ROWS:(k + 1) * ROWS, earlier + i:earlier + i + 1], (ROWS, LANES)
            )
            for i in range(k + 1)
        ]
        for k in range(block)
    ]
    for c in range(comp):
        out = dot_pieces(mix, [pieces[at, c] for at in range(3)])
        for x in range(width):
            for k in range(block):
                value = out[k * ROWS:(k + 1) * ROWS, LANES * x:LANES * (x + 1)]
                for i in range(k + 1):
                    value = value + weights[k][i] * allv[earlier + i, c, x]
                new_ref[k, c, x] = value

    @pl.loop(0, depth)
    def _(step):
        for kind in (0, 1):
            for side in (0, 1):
                @pl.when(has(kind, side, True))
                def _():
                    halo_copy(step, kind, side).wait_send()

    for kind in (0, 1):
        for at, stage in enumerate(stages):
            for offset in range(1, stage[2]):
                move(kind, at, offset, True).wait_send()


def hand_over(rows, new_in, small, new_out, proj_out, tri_out):
    new_out[...] = new_in[...]
    proj_out[...] = small[: proj_out.shape[0], : proj_out.shape[1]]
    tri_out[...] = small[rows:rows + tri_out.shape[0], : tri_out.shape[1]]


def body(sizes, coefficients, earlier, start, shifts):
    coefficients = jnp.transpose(coefficients, (0, 1, 2, 4, 3, 5))
    earlier = jnp.transpose(earlier, (0, 1, 3, 2, 4))
    start = jnp.transpose(start, (0, 2, 1, 3))
    depth, count = shifts.shape[0], earlier.shape[0]
    block = depth + 1
    kinds, comp, _, width, rows, lanes = coefficients.shape
    stages = stages_of(sizes)
    most = max(stage[2] for stage in stages)
    f32 = jnp.float32
    anywhere = pl.BlockSpec(memory_space=pl.ANY)
    vmem = pl.BlockSpec(memory_space=pltpu.VMEM)
    new, small = pl.pallas_call(
        functools.partial(kernel, sizes),
        out_shape=(
            jax.ShapeDtypeStruct((block, comp, width, rows, lanes), f32),
            jax.ShapeDtypeStruct((2 * rows, lanes), f32),
        ),
        in_specs=[anywhere, anywhere, anywhere, pl.BlockSpec(memory_space=pltpu.SMEM)],
        out_specs=(vmem, vmem),
        scratch_shapes=[
            pltpu.VMEM(coefficients.shape, coefficients.dtype),
            pltpu.VMEM(coefficients.shape, f32),
            pltpu.VMEM((comp, comp, rows, lanes), f32),
            pltpu.VMEM((count + block, comp, width, rows, lanes), f32),
            pltpu.VMEM((3, comp, count * rows, width * lanes), jnp.bfloat16),
            pltpu.VMEM((comp, width, rows, lanes), f32),
            pltpu.VMEM((depth, 2, comp, rows, lanes), f32),
            pltpu.VMEM((depth, 2, 4 * comp, lanes), f32),
            pltpu.VMEM((depth, 2, 4 * comp, lanes), f32),
            pltpu.VMEM((count * rows, count * rows), f32),
            pltpu.VMEM((lanes, lanes), f32),
            pltpu.VMEM((rows, lanes), f32),
            pltpu.VMEM((len(stages) + 1, rows // 2, lanes), f32),
            pltpu.VMEM((len(stages), most, rows // 2, lanes), f32),
            pltpu.VMEM((len(stages) + 1, rows, lanes), f32),
            pltpu.VMEM((len(stages), most, rows, lanes), f32),
            pltpu.SemaphoreType.DMA((3,)),
            pltpu.SemaphoreType.DMA((depth, 2, 2)),
            pltpu.SemaphoreType.DMA((depth, 2, 2)),
            pltpu.SemaphoreType.DMA((2, len(stages), most)),
            pltpu.SemaphoreType.DMA((2, len(stages), most)),
        ],
        compiler_params=pltpu.CompilerParams(collective_id=0, has_side_effects=True),
        name="powers",
    )(coefficients, earlier, start, shifts)
    new, proj, tri = pl.pallas_call(
        functools.partial(hand_over, rows),
        out_shape=(
            jax.ShapeDtypeStruct(new.shape, f32),
            jax.ShapeDtypeStruct((block, count), f32),
            jax.ShapeDtypeStruct((block, block), f32),
        ),
        in_specs=[vmem, vmem],
        out_specs=(vmem, vmem, vmem),
        name="hand_over",
    )(new, small)
    return jnp.transpose(new, (0, 1, 3, 2, 4)), proj.T, tri


def solution(mesh):
    sizes = (("slab", mesh.shape["slab"]), ("sub", mesh.shape["sub"]))
    placed = (
        P(None, None, None, "slab", "sub", None),
        P(None, None, "slab", "sub", None),
        P(None, "slab", "sub", None),
        P(),
    )
    return jax.shard_map(
        functools.partial(body, sizes),
        mesh=mesh,
        in_specs=placed,
        out_specs=(P(None, None, "slab", "sub", None), P(), P()),
        check_vma=False,
    )
```

profile of v0, /device:TPU:0, one launch (start us, length us, event | category | flops | bytes accessed | tf_op | source)
XLA Modules:
  0.0 35.4 jit_solution(9356264669045934922)
XLA Ops:
  0.6 32.9 %powers.1 = (f32[6,6,3,8,128]{4,3,2,1,0:T(8,128)}, f32[16,128]{1,0:T(8,128)}) custom-call(bf16[7,6,6,3,8,128]{5,4,3,2,1,0:T(8,128)(2,1)} %bitcast.6, f32[30,6,3,8,128]{4,3,2,1,0:T(8,128)} %bitcast.5, f32[6,3,8,128]{3,2,1,0:T(8,128)} %bitcast.7, f32[5]{0:T(128)} %shifts_ref.1), custom_call_target="tpu_custom_call" | custom-call | tf_op jit(solution)/shard_map/powers/pallas_call | solution.py:432
  33.6 1.8 %hand_over.1 = (f32[6,6,3,8,128]{4,3,2,1,0:T(8,128)}, f32[6,30]{1,0:T(8,128)}, f32[6,6]{1,0:T(8,128)}) custom-call(f32[6,6,3,8,128]{4,3,2,1,0:T(8,128)} %get-tuple-element.8.new_in, f32[16,128]{1,0:T(8,128)} %get-tuple-element.9.small), custom_call_target="tpu_custom_call" | custom-call | tf_op jit(solution)/shard_map/hand_over/pallas_call | solution.py:466
where the time goes:
time: 35.5 us; the launch traced here: 35.4 us
  Pallas kernels  34.7 us (98%)
  between operations  0.64 us (2%)
    pallas_call x1, Pallas kernels, body(): pl.pallas_call(functools.partial(kernel, sizes), out_shape=(jax.ShapeDtyp...  32.9 us
    pallas_call x1, Pallas kernels, body(): pl.pallas_call(functools.partial(hand_over, rows), out_shape=(jax.ShapeDt...  1.81 us

commit v1 on v0

v1 whole, which is shorter than its diff:
```python
import functools

import jax
import jax.numpy as jnp
from jax import lax
from jax.experimental import pallas as pl
from jax.experimental.pallas import tpu as pltpu
from jax.sharding import PartitionSpec as P

MESH = pl.DeviceIdType.MESH
LANES = 128
ROWS = 8


def dot(a, b, nt=False):
    return lax.dot_general(
        a, b, (((1,), (1 if nt else 0,)), ((), ())),
        precision=lax.Precision.HIGHEST, preferred_element_type=jnp.float32,
    )


def iota(shape, dim):
    return lax.broadcasted_iota(jnp.int32, shape, dim)


def onehot(shape, test):
    return jnp.where(test(iota(shape, 0), iota(shape, 1)), 1.0, 0.0).astype(jnp.float32)


def diagonal(value):
    r, q = iota(value.shape, 0), iota(value.shape, 1)
    return jnp.where((r & 7) == (q & 7), value, 0.0)


def split(value):
    first = value.astype(jnp.bfloat16)
    left = value - first.astype(jnp.float32)
    second = left.astype(jnp.bfloat16)
    third = (left - second.astype(jnp.float32)).astype(jnp.bfloat16)
    return [first, second, third]


def dot_pieces(a, b, nt=False):
    found = None
    rows = a[0].shape[0]
    for at in (2, 1, 0):
        left = jnp.concatenate(a[: 3 - at], axis=0)
        part = lax.dot_general(
            left, b[at], (((1,), (1 if nt else 0,)), ((), ())),
            preferred_element_type=jnp.float32,
        )
        for i in reversed(range(3 - at)):
            piece = part[i * rows:(i + 1) * rows]
            found = piece if found is None else found + piece
    return found


def side_by_side(value):
    count, width = value.shape[0], value.shape[1]
    return jnp.concatenate(
        [value[:, x].reshape(count * ROWS, LANES) for x in range(width)], axis=1
    )


def factors(count):
    found = []
    while count > 1:
        fits = [f for f in range(2, min(count, 8) + 1) if count % f == 0]
        found.append(max(fits) if fits else count)
        count //= found[-1]
    return found


def stages_of(sizes):
    found = []
    for at, (_, count) in enumerate(sizes):
        stride = 1
        for size in factors(count):
            found.append(((stride, size), (1, 1)) if at == 0 else ((1, 1), (stride, size)))
            stride *= size
    return found


def joint_stages_of(sizes):
    slabs, subs = stages_of(sizes[:1]), [s[1] for s in stages_of((("", 1), sizes[1]))]
    first = slabs[0][0] if slabs else (1, 1)
    found = [(first, subs[0] if subs else (1, 1))]
    found += [(s[0], (1, 1)) for s in slabs[1:]] + [((1, 1), s) for s in subs[1:]]
    return found


def members(stage):
    return stage[0][1] * stage[1][1]


def offsets_of(stage):
    return [(a, b) for a in range(stage[0][1]) for b in range(stage[1][1]) if a or b]


def steps_of(depth):
    return ([1] if depth % 2 else []) + [2] * (depth // 2)


def lane_sums(value):
    return jnp.sum(value, axis=1, keepdims=True)


def sublane_sums(value):
    for shift in (4, 2, 1):
        value = value + pltpu.roll(value, shift, 0)
    return value


def inverse_root(value):
    scale = lax.rsqrt(value)
    return scale * (1.5 - 0.5 * value * scale * scale)


def kernel(
    sizes, coef_hbm, early_hbm, start_hbm, shifts_ref, new_ref, small_ref,
    coef_in, coef, edge_coef, gx_in, gz_send, gz_in, gz, allv, pieces, part, acc_ref,
    halo_x, halo_z, send_z, send_c, halo_c, pre_x, pre_z, ghost_x, ghost_z,
    ee, sums_ref, late_ref,
    mine_ee, gathered_ee, mine_b, gathered_b, mine_f, gathered_f,
    in_sem, face_send, face_recv, corner_send, corner_recv, g_send, g_recv,
    ee_send, ee_recv, b_send, b_recv, f_send, f_recv,
):
    depth = shifts_ref.shape[0]
    earlier, comp, width = early_hbm.shape[:3]
    block = depth + 1
    count = comp * width * ROWS * LANES * sizes[0][1] * sizes[1][1]
    half = LANES // 2
    rounds = steps_of(depth)
    single = stages_of(sizes)
    joint = joint_stages_of(sizes)
    place = [lax.axis_index(axis) for axis, _ in sizes]
    extent = [n for _, n in sizes]
    names = [axis for axis, _ in sizes]
    late = block - rounds[-1]
    lines = late // 2 + late % 2

    copy_start = pltpu.make_async_copy(start_hbm, allv.at[earlier], in_sem.at[0])
    copy_coef = pltpu.make_async_copy(coef_hbm, coef_in, in_sem.at[1])
    copy_early = pltpu.make_async_copy(early_hbm, allv.at[pl.ds(0, earlier)], in_sem.at[2])
    copy_start.start()
    copy_coef.start()
    copy_early.start()

    halo_x[...] = jnp.zeros_like(halo_x)
    halo_z[...] = jnp.zeros_like(halo_z)
    halo_c[...] = jnp.zeros_like(halo_c)
    gx_in[...] = jnp.zeros_like(gx_in)
    gz_in[...] = jnp.zeros_like(gz_in)

    def there(kind, side, sending):
        upward = (side == 0) == sending
        return place[kind] < extent[kind] - 1 if upward else place[kind] > 0

    def at_peer(dz, dx):
        return {names[0]: place[0] + dz, names[1]: place[1] + dx}

    def toward(side):
        return 1 if side == 0 else -1

    def peer(stage, offset):
        mine_at, peer_at, target = [], [], {}
        for axis in (0, 1):
            stride, size = stage[axis]
            digit = lax.rem(place[axis] // stride, size)
            other = lax.rem(digit + offset[axis], size)
            mine_at.append(digit)
            peer_at.append(other)
            target[names[axis]] = place[axis] + (other - digit) * stride
        flat = stage[1][1]
        return mine_at[0] * flat + mine_at[1], peer_at[0] * flat + peer_at[1], target

    barrier = pltpu.get_barrier_semaphore()
    expected = 0
    for stage in single + joint:
        for offset in offsets_of(stage):
            _, _, target = peer(stage, offset)
            pl.semaphore_signal(barrier, inc=1, device_id=target, device_id_type=MESH)
            expected += 1
    around = [(dz, dx) for dz in (-1, 0, 1) for dx in (-1, 0, 1) if dz or dx]
    beyond = around if len(joint) > 1 else []

    def exists(dz, dx):
        a = place[0] + dz
        b = place[1] + dx
        return (a >= 0) & (a < extent[0]) & (b >= 0) & (b < extent[1])

    for dz, dx in beyond:
        @pl.when(exists(dz, dx))
        def _():
            pl.semaphore_signal(barrier, inc=1, device_id=at_peer(dz, dx), device_id_type=MESH)

    send_z[...] = jnp.zeros_like(send_z)
    send_c[...] = jnp.zeros_like(send_c)
    edge_coef[...] = jnp.zeros_like(edge_coef)
    ee[...] = jnp.zeros_like(ee)
    sums_ref[...] = jnp.zeros_like(sums_ref)
    late_ref[...] = jnp.zeros_like(late_ref)

    def face_copy(r, step, what, kind, side):
        if kind == 0:
            src, dst = send_z.at[r, what, side], halo_z.at[r, what, side]
        else:
            x = width - 1 if side == 0 else 0
            src = allv.at[earlier + step, :, x] if what == 0 else part.at[r, :, x]
            dst = halo_x.at[r, what, side]
        dz, dx = (toward(side), 0) if kind == 0 else (0, toward(side))
        return pltpu.make_async_remote_copy(
            src_ref=src, dst_ref=dst,
            send_sem=face_send.at[r, what, kind, side],
            recv_sem=face_recv.at[r, what, kind, side],
            device_id=at_peer(dz, dx), device_id_type=MESH,
        )

    def corner_copy(r, sz, sx):
        return pltpu.make_async_remote_copy(
            src_ref=send_c.at[r, sz, sx], dst_ref=halo_c.at[r, sz, sx],
            send_sem=corner_send.at[r, sz, sx], recv_sem=corner_recv.at[r, sz, sx],
            device_id=at_peer(toward(sz), toward(sx)), device_id_type=MESH,
        )

    def g_copy(kind, side):
        if kind == 0:
            src, dst = gz_send.at[side], gz_in.at[side]
        else:
            src = coef_in.at[4, :, :, width - 1] if side == 0 else coef_in.at[3, :, :, 0]
            dst = gx_in.at[side]
        dz, dx = (toward(side), 0) if kind == 0 else (0, toward(side))
        return pltpu.make_async_remote_copy(
            src_ref=src, dst_ref=dst, send_sem=g_send.at[kind, side],
            recv_sem=g_recv.at[kind, side], device_id=at_peer(dz, dx), device_id_type=MESH,
        )

    def each_face(sending, kinds, act):
        for kind in kinds:
            for side in (0, 1):
                @pl.when(there(kind, side, sending))
                def _():
                    act(kind, side)

    def each_corner(sending, act):
        for sz in (0, 1):
            for sx in (0, 1):
                @pl.when(there(0, sz, sending) & there(1, sx, sending))
                def _():
                    act(sz, sx)

    def pack(r, what, source):
        for e in range(comp):
            for x in range(width):
                row = 4 * e + x
                tile = source(e, x)
                send_z[r, what, 0, row:row + 1, :] = tile[ROWS - 1:ROWS, :]
                send_z[r, what, 1, row:row + 1, :] = tile[0:1, :]

    def send_faces(r, step):
        pack(r, 0, lambda e, x: allv.at[earlier + step, e, x])
        each_face(True, (0, 1), lambda kind, side: face_copy(r, step, 0, kind, side).start())

    row2 = iota((ROWS, LANES), 0)
    row3 = iota((width, ROWS, LANES), 1)
    lane3 = iota((width, ROWS, LANES), 2)
    zero_tile = jnp.zeros((1, ROWS, LANES), jnp.float32)
    low_rows = row2 < 4

    def split_pair(below, above, odd):
        if odd:
            return jnp.where(low_rows, pltpu.roll(below, 4, 0), above)
        return jnp.where(low_rows, below, pltpu.roll(above, 4, 0))

    def pair_tile(ref, index, e):
        base = ROWS * (e // 2)
        return split_pair(
            ref[(*index, 0, slice(base, base + ROWS))],
            ref[(*index, 1, slice(base, base + ROWS))], e % 2,
        )

    def apply_local(step):
        acc = (1.0 - shifts_ref[step]) * allv[earlier + step]
        for e in range(comp):
            v = allv[earlier + step, e]
            near = [
                v,
                jnp.where(row3 > 0, pltpu.roll(v, 1, 1), 0.0),
                jnp.where(row3 < ROWS - 1, pltpu.roll(v, ROWS - 1, 1), 0.0),
                jnp.concatenate([zero_tile, v[:-1]], axis=0),
                jnp.concatenate([v[1:], zero_tile], axis=0),
                jnp.where(lane3 > 0, pltpu.roll(v, 1, 2), 0.0),
                jnp.where(lane3 < LANES - 1, pltpu.roll(v, LANES - 1, 2), 0.0),
            ]
            for d in range(len(near)):
                acc = acc + coef[d, :, e] * near[d][None]
        return acc

    def add_x(source, x_of):
        found = []
        for side, d, x in ((0, 3, 0), (1, 4, width - 1)):
            value = source(x)
            for e in range(comp):
                value = value + coef[d, :, e, x] * x_of(side, e)[None]
            found.append(value)
        return found

    def add_z(z_of):
        edge = jnp.zeros((comp, ROWS, LANES), jnp.float32)
        for e in range(comp):
            edge = edge + edge_coef[:, e] * z_of(e)[None]
        return edge

    def store_step(step, source, sides, edge):
        for c in range(comp):
            for x in range(width):
                value = sides[0][c] if x == 0 else sides[1][c] if x == width - 1 else source(x)[c]
                value = value + jnp.where(
                    row2 == 0, edge[c, x:x + 1, :],
                    jnp.where(row2 == ROWS - 1, edge[c, 4 + x:5 + x, :], 0.0),
                )
                allv[earlier + step, c, x] = value

    def take_faces(r, step, source):
        each_face(False, (1,), lambda kind, side: face_copy(r, step, 0, kind, side).wait_recv())
        sides = add_x(source, lambda side, e: halo_x[r, 0, side, e])
        each_face(False, (0,), lambda kind, side: face_copy(r, step, 0, kind, side).wait_recv())
        edge = add_z(lambda e: pair_tile(halo_z, (r, 0), e))
        store_step(step + 1, source, sides, edge)

    def cross_products(k, ref, base):
        total, group = earlier + k + 1, 6
        w = allv[earlier + k]
        for low in range(0, total, group):
            high = min(low + group, total)
            sums = jnp.sum(w[None] * allv[low:high], axis=(1, 2))
            ref[base + low:base + high, :] = jnp.sum(sums, axis=1)

    def as_line(value):
        return jnp.sum(value.T, axis=0, keepdims=True)

    def self_products(c):
        parts = split(side_by_side(allv[pl.ds(0, earlier), c]))
        for at, piece in enumerate(parts):
            pieces[at, c] = piece
        ee[...] += dot_pieces(parts, [parts[0], parts[1], parts[2]], nt=True)

    def self_finish():
        span = earlier * ROWS
        wide = dot(diagonal(ee[...]), onehot((span, LANES), lambda r, q: (r >> 3) == (q & 31)))
        wide = jnp.where((iota(wide.shape, 0) >> 6) == (iota(wide.shape, 1) >> 5), wide, 0.0)
        mine_ee[0] = dot(onehot((ROWS, span), lambda r, q: ((q >> 3) & 7) == r), wide)

    exchanges = {
        "ee": (single, mine_ee, gathered_ee, ee_send, ee_recv),
        "b": (joint, mine_b, gathered_b, b_send, b_recv),
        "f": (joint, mine_f, gathered_f, f_send, f_recv),
    }

    def begin(name, at):
        stages, own, slots, send_sem, recv_sem = exchanges[name]
        for offset in offsets_of(stages[at]):
            here, other, target = peer(stages[at], offset)
            pltpu.make_async_remote_copy(
                src_ref=own.at[at], dst_ref=slots.at[at, here],
                send_sem=send_sem.at[at, other], recv_sem=recv_sem.at[at, here],
                device_id=target, device_id_type=MESH,
            ).start()

    def finish(name, at):
        stages, own, slots, send_sem, recv_sem = exchanges[name]
        here, _, _ = peer(stages[at], (0, 0))
        slots[at, here] = own[at]
        for offset in offsets_of(stages[at]):
            _, other, target = peer(stages[at], offset)
            pltpu.make_async_remote_copy(
                src_ref=own.at[at], dst_ref=slots.at[at, other],
                send_sem=send_sem.at[at, other], recv_sem=recv_sem.at[at, other],
                device_id=target, device_id_type=MESH,
            ).wait_recv()
        whole = slots[at, 0]
        for other in range(1, members(stages[at])):
            whole = whole + slots[at, other]
        own[at + 1] = whole

    def drain(name):
        stages, own, slots, send_sem, recv_sem = exchanges[name]
        for at, stage in enumerate(stages):
            for offset in offsets_of(stage):
                here, other, target = peer(stage, offset)
                pltpu.make_async_remote_copy(
                    src_ref=own.at[at], dst_ref=slots.at[at, here],
                    send_sem=send_sem.at[at, other], recv_sem=recv_sem.at[at, here],
                    device_id=target, device_id_type=MESH,
                ).wait_send()

    def whole_exchange(name, first):
        stages = exchanges[name][0]
        for at in range(len(stages)):
            if at or not first:
                begin(name, at)
            finish(name, at)
        return exchanges[name][1][len(stages)] * (1.0 / count)

    def load_coefficients():
        @pl.loop(0, comp)
        def _(c):
            for d in range(coef.shape[0]):
                coef[d, c] = coef_in[d, c].astype(jnp.float32)
            for e in range(comp):
                for x in range(width):
                    edge_coef[c, e, x:x + 1, :] = coef[1, c, e, x, 0:1, :]
                    edge_coef[c, e, 4 + x:5 + x, :] = coef[2, c, e, x, ROWS - 1:ROWS, :]

        flat = comp * comp // 2
        for low in range(0, flat, 2):
            for side in (0, 1):
                both = []
                for at in (low, low + 1):
                    c, e = 2 * at // comp, 2 * at % comp
                    one, two = edge_coef[c, e], edge_coef[c, e + 1]
                    if side == 0:
                        both.append(jnp.where(low_rows, pltpu.roll(one, 4, 0), two))
                    else:
                        both.append(jnp.where(low_rows, one, pltpu.roll(two, 4, 0)))
                gz_send[side, ROWS * low:ROWS * (low + 2), :] = jnp.concatenate(
                    both, axis=0
                ).astype(jnp.bfloat16)

    def take_couplings():
        each_face(False, (0, 1), lambda kind, side: g_copy(kind, side).wait_recv())
        for low in range(0, comp * comp // 2, 2):
            below = gz_in[0, ROWS * low:ROWS * (low + 2), :].astype(jnp.float32)
            above = gz_in[1, ROWS * low:ROWS * (low + 2), :].astype(jnp.float32)
            for at in (0, 1):
                c, e = 2 * (low + at) // comp, 2 * (low + at) % comp
                b, a = below[ROWS * at:ROWS * (at + 1)], above[ROWS * at:ROWS * (at + 1)]
                gz[c, e] = split_pair(b, a, 0)
                gz[c, e + 1] = split_pair(b, a, 1)

    def complete_neighbours(r, step):
        for side, x in ((0, 0), (1, width - 1)):
            for c in range(comp):
                value = jnp.zeros((ROWS, LANES), jnp.float32)
                for e in range(comp):
                    value = value + gx_in[side, c, e].astype(jnp.float32) * allv[earlier + step, e, x]
                pre_x[side, c] = value
        total = jnp.zeros((comp, ROWS, LANES), jnp.float32)
        for e in range(comp):
            base = ROWS * (e // 2)
            own = split_pair(
                send_z[r, 0, 1, base:base + ROWS, :], send_z[r, 0, 0, base:base + ROWS, :], e % 2
            )
            total = total + gz[:, e] * own[None]
        pre_z[...] = total
        for sz in (0, 1):
            for sx in (0, 1):
                z = ROWS - 1 if sz == 0 else 0
                x = (4 if sz == 0 else 0) + (width - 1 if sx == 0 else 0)
                for c in range(comp):
                    send_c[r, sz, sx, c:c + 1, :] = pre_x[1 - sx, c, z:z + 1, :]
                    send_c[r, sz, sx, ROWS + c:ROWS + c + 1, :] = pre_z[c, x:x + 1, :]
        each_corner(True, lambda sz, sx: corner_copy(r, sz, sx).start())

    def take_ghosts(r, step):
        each_face(False, (1, 0), lambda kind, side: face_copy(r, step, 1, kind, side).wait_recv())
        each_corner(False, lambda sz, sx: corner_copy(r, sz, sx).wait_recv())
        for c in range(comp):
            value = pair_tile(halo_z, (r, 1), c) + pre_z[c]
            for sz in (0, 1):
                for sx in (0, 1):
                    row = (0 if sz == 0 else 4) + (0 if sx == 0 else width - 1)
                    value = value + jnp.where(row2 == row, halo_c[r, sz, sx, c:c + 1, :], 0.0)
            ghost_z[c] = value
            for side in (0, 1):
                value = halo_x[r, 1, side, c] + pre_x[side, c]
                for sz in (0, 1):
                    row = 0 if sz == 0 else ROWS - 1
                    value = value + jnp.where(
                        row2 == row, halo_c[r, sz, side, ROWS + c:ROWS + c + 1, :], 0.0
                    )
                ghost_x[side, c] = value

    copy_start.wait()
    for dz, dx in beyond:
        @pl.when(exists(dz, dx))
        def _():
            pl.semaphore_wait(barrier, 1)
    pl.semaphore_wait(barrier, expected)

    step = 0
    comps = list(range(comp))
    paired = [r for r, size in enumerate(rounds) if size == 2]
    per_round = -(-comp // max(1, len(rounds) - 1))
    done = 0
    ee_begun = False
    for r, size in enumerate(rounds):
        send_faces(r, step)
        if r == 0:
            copy_coef.wait()
            load_coefficients()
            each_face(True, (0, 1), lambda kind, side: g_copy(kind, side).start())
        if size == 2 and r == paired[0]:
            take_couplings()
        if size == 2:
            complete_neighbours(r, step)
        part[r] = apply_local(step)
        if size == 2:
            pack(r, 1, lambda e, x: part.at[r, e, x])
            each_face(True, (0, 1), lambda kind, side: face_copy(r, step, 1, kind, side).start())
        if r == 0:
            copy_early.wait()
        for k in range(done, min(step + 1, late)):
            cross_products(k, sums_ref.at[k // 2], (k % 2) * half)
            done = k + 1
        if done == late and r == len(rounds) - 1:
            for q in range(lines):
                mine_b[0, q] = as_line(sums_ref[q])
            begin("b", 0)
        todo, comps = comps[:per_round], comps[per_round:]
        if todo:
            @pl.loop(todo[0], todo[-1] + 1)
            def _(c):
                self_products(c)
        if ee_begun:
            finish("ee", 0)
            if len(single) > 1:
                begin("ee", 1)
            ee_begun = False
        if todo and not comps:
            self_finish()
            begin("ee", 0)
            ee_begun = len(rounds) - 1 > r
        take_faces(r, step, lambda x, r=r: part[r, :, x])
        if size == 2:
            if r == len(rounds) - 1:
                cross_products(step + 1, late_ref, 0)
            acc_ref[...] = apply_local(step + 1)
            take_ghosts(r, step)
            sides = add_x(lambda x: acc_ref[:, x], lambda side, e: ghost_x[side, e])
            edge = add_z(lambda e: ghost_z[e])
            store_step(step + 2, lambda x: acc_ref[:, x], sides, edge)
        step += size

    cross_products(depth, late_ref, half)
    mine_f[0] = as_line(late_ref[...])
    begin("f", 0)

    ee_from = 1 if len(single) > 1 else 0
    for at in range(ee_from, len(single)):
        if at > ee_from:
            begin("ee", at)
        finish("ee", at)
    packed = mine_ee[len(single)] * (1.0 / count)
    early = whole_exchange("b", True)

    row, lane = iota((ROWS, LANES), 0), iota((ROWS, LANES), 1)
    found = jnp.concatenate(
        [
            early[k // 2] if k % 2 == 0 else pltpu.roll(early[k // 2], half, 1)
            for k in range(late)
        ] + [jnp.zeros((ROWS - late, LANES), jnp.float32)], axis=0
    )
    proj_t = jnp.where(lane < earlier, found, 0.0)
    known = jnp.where(lane < earlier + row, found, 0.0)
    pick = onehot((ROWS, LANES), lambda r, q: q == r + earlier)
    gram = jnp.where(lane <= earlier + row, found, 0.0)
    gram = pltpu.roll(gram, LANES - earlier, 1)[:, :ROWS]
    square = jnp.concatenate(
        [packed] + [pltpu.roll(packed, LANES - 32 * g, 1) for g in range(1, 4)], axis=0
    )
    sr, sl = iota(square.shape, 0), iota(square.shape, 1)
    inside = (sl < earlier) & (sr < earlier)
    square = jnp.where(inside, square - jnp.where(sr == sl, 2.0, 0.0), 0.0)
    moved = dot(proj_t[:, :32], square) + pick
    gram = gram + dot(moved, known, nt=True)

    upper = gram
    inverse = onehot((ROWS, ROWS), lambda r, q: (r == q) & (r < late))
    r8 = iota((ROWS, ROWS), 0)
    q8 = iota((ROWS, ROWS), 1)
    for p in range(late):
        pivot = upper[p:p + 1, p:p + 1]
        scale = inverse_root(pivot)
        column = upper[:, p:p + 1] * scale
        row_u, row_i = upper[p:p + 1, :] * scale, inverse[p:p + 1, :] * scale
        upper = jnp.where(r8 == p, row_u, jnp.where(r8 > p, upper - column * row_u, upper))
        inverse = jnp.where(r8 == p, row_i, jnp.where(r8 > p, inverse - column * row_i, inverse))
    onto = dot(inverse, moved)

    mix = dot(inverse, pick - proj_t)
    tall = dot(onehot((late * ROWS, ROWS), lambda r, q: (r >> 3) == q), mix)
    span = earlier * ROWS
    mix = split(diagonal(dot(tall, onehot((LANES, span), lambda r, q: (q >> 3) == r))))
    weights = [
        [
            jnp.broadcast_to(
                tall[k * ROWS:(k + 1) * ROWS, earlier + i:earlier + i + 1], (ROWS, LANES)
            )
            for i in range(k + 1)
        ]
        for k in range(late)
    ]
    for c in range(comp):
        out = dot_pieces(mix, [pieces[at, c] for at in range(3)])
        for x in range(width):
            for k in range(late):
                value = out[k * ROWS:(k + 1) * ROWS, LANES * x:LANES * (x + 1)]
                for i in range(k + 1):
                    value = value + weights[k][i] * allv[earlier + i, c, x]
                new_ref[k, c, x] = value
    small_ref[0:ROWS, :] = proj_t
    small_ref[ROWS:2 * ROWS, :] = jnp.zeros((ROWS, LANES), jnp.float32)
    small_ref[ROWS:2 * ROWS, 0:ROWS] = jnp.where((q8 >= r8) & (r8 < late), upper, 0.0)

    final = whole_exchange("f", True)
    ys = [final, pltpu.roll(final, half, 1)][2 - (block - late):]
    spread = [jnp.broadcast_to(y, (ROWS, LANES)) for y in ys]
    tiles = -(-(earlier + block) // ROWS)
    columns = []
    for y in spread:
        col = [
            lane_sums(jnp.where(lane == row + ROWS * t, y, 0.0)) for t in range(tiles)
        ]
        img = [
            lane_sums(square[ROWS * t:ROWS * (t + 1)] * y) for t in range(square.shape[0] // ROWS)
        ]
        columns.append((col, img, lane_sums(onto * y)))
    wide = lambda value: jnp.broadcast_to(value, (ROWS, LANES))

    def inner(a, b):
        (col_a, _, r_a), (col_b, img_b, r_b) = columns[a], columns[b]
        total = -(r_a * r_b)
        for t in range(len(img_b)):
            total = total + jnp.where(row[:, :1] + ROWS * t < earlier, col_a[t] * img_b[t], 0.0)
        for t in range(tiles):
            total = total + jnp.where(row[:, :1] + ROWS * t == earlier + late + a, col_b[t], 0.0)
        return sublane_sums(wide(total))

    fresh = block - late
    scales, ratios, lines_out = [], {}, []
    for b in range(fresh):
        value = inner(b, b)
        for a in range(b):
            cross = inner(a, b)
            ratios[a, b] = cross * scales[a]
            value = value - ratios[a, b] * ratios[a, b]
        scales.append(inverse_root(value))
        ratios[b, b] = value * scales[b]
    triangle = small_ref[ROWS:2 * ROWS, :]
    proj_rows = small_ref[0:ROWS, :]
    for b in range(fresh):
        k = late + b
        triangle = triangle + jnp.where(lane == k, wide(columns[b][2]), 0.0)
        for a in range(b + 1):
            triangle = triangle + jnp.where((lane == k) & (row == late + a), ratios[a, b], 0.0)
        proj_rows = jnp.where((row == k) & (lane < earlier), spread[b], proj_rows)
    small_ref[ROWS:2 * ROWS, :] = triangle
    small_ref[0:ROWS, :] = proj_rows
    for b in range(fresh):
        for t in range(tiles):
            late_ref[b * half + ROWS * t:b * half + ROWS * (t + 1), :] = wide(columns[b][0][t])
        late_ref[b * half + ROWS * tiles:b * half + ROWS * (tiles + 1), :] = wide(columns[b][2])

    for c in range(comp):
        totals = [allv[earlier + late + b, c] for b in range(fresh)]
        for j in range(earlier):
            v = allv[j, c]
            for b in range(fresh):
                at = b * half + j
                totals[b] = totals[b] - late_ref[at:at + 1, :] * v
        for i in range(late):
            v = new_ref[i, c]
            for b in range(fresh):
                at = b * half + ROWS * tiles + i
                totals[b] = totals[b] - late_ref[at:at + 1, :] * v
        outs = []
        for b in range(fresh):
            value = totals[b]
            for a in range(b):
                value = value - ratios[a, b] * outs[a]
            outs.append(value * scales[b])
            new_ref[late + b, c] = outs[b]

    step = 0
    for r, size in enumerate(rounds):
        for what in range(size):
            each_face(
                True, (0, 1),
                lambda kind, side: face_copy(r, step, what, kind, side).wait_send(),
            )
        if size == 2:
            each_corner(True, lambda sz, sx: corner_copy(r, sz, sx).wait_send())
        step += size
    each_face(True, (0, 1), lambda kind, side: g_copy(kind, side).wait_send())
    for name in exchanges:
        drain(name)


def hand_over(rows, new_in, small, new_out, proj_out, tri_out, sem):
    copy = pltpu.make_async_copy(new_in, new_out, sem.at[0])
    copy.start()
    proj_out[...] = small[: proj_out.shape[0], : proj_out.shape[1]]
    tri_out[...] = small[rows:rows + tri_out.shape[0], : tri_out.shape[1]]
    copy.wait()


def body(sizes, coefficients, earlier, start, shifts):
    coefficients = jnp.transpose(coefficients, (0, 1, 2, 4, 3, 5))
    earlier = jnp.transpose(earlier, (0, 1, 3, 2, 4))
    start = jnp.transpose(start, (0, 2, 1, 3))
    depth, count = shifts.shape[0], earlier.shape[0]
    block = depth + 1
    kinds, comp, _, width, rows, lanes = coefficients.shape
    rounds = len(steps_of(depth))
    late = block - steps_of(depth)[-1]
    lines = late // 2 + late % 2
    single, joint = stages_of(sizes), joint_stages_of(sizes)
    most = max(members(stage) for stage in single)
    joined = max(members(stage) for stage in joint)
    f32, b16 = jnp.float32, jnp.bfloat16
    anywhere = pl.BlockSpec(memory_space=pl.ANY)
    vmem = pl.BlockSpec(memory_space=pltpu.VMEM)
    sems = pltpu.SemaphoreType.DMA
    new, small = pl.pallas_call(
        functools.partial(kernel, sizes),
        out_shape=(
            pltpu.VMEM((block, comp, width, rows, lanes), f32),
            pltpu.VMEM((2 * rows, lanes), f32),
        ),
        in_specs=[anywhere, anywhere, anywhere, pl.BlockSpec(memory_space=pltpu.SMEM)],
        out_specs=(vmem, vmem),
        scratch_shapes=[
            pltpu.VMEM(coefficients.shape, coefficients.dtype),
            pltpu.VMEM(coefficients.shape, f32),
            pltpu.VMEM((comp, comp, rows, lanes), f32),
            pltpu.VMEM((2, comp, comp, rows, lanes), b16),
            pltpu.VMEM((2, 4 * comp * comp, lanes), b16),
            pltpu.VMEM((2, 4 * comp * comp, lanes), b16),
            pltpu.VMEM((comp, comp, rows, lanes), f32),
            pltpu.VMEM((count + block, comp, width, rows, lanes), f32),
            pltpu.VMEM((3, comp, count * rows, width * lanes), b16),
            pltpu.VMEM((rounds, comp, width, rows, lanes), f32),
            pltpu.VMEM((comp, width, rows, lanes), f32),
            pltpu.VMEM((rounds, 2, 2, comp, rows, lanes), f32),
            pltpu.VMEM((rounds, 2, 2, 4 * comp, lanes), f32),
            pltpu.VMEM((rounds, 2, 2, 4 * comp, lanes), f32),
            pltpu.VMEM((rounds, 2, 2, 2 * rows, lanes), f32),
            pltpu.VMEM((rounds, 2, 2, 2 * rows, lanes), f32),
            pltpu.VMEM((2, comp, rows, lanes), f32),
            pltpu.VMEM((comp, rows, lanes), f32),
            pltpu.VMEM((2, comp, rows, lanes), f32),
            pltpu.VMEM((comp, rows, lanes), f32),
            pltpu.VMEM((count * rows, count * rows), f32),
            pltpu.VMEM((lines, lanes, lanes), f32),
            pltpu.VMEM((lanes, lanes), f32),
            pltpu.VMEM((len(single) + 1, rows, lanes), f32),
            pltpu.VMEM((len(single), most, rows, lanes), f32),
            pltpu.VMEM((len(joint) + 1, lines, 1, lanes), f32),
            pltpu.VMEM((len(joint), joined, lines, 1, lanes), f32),
            pltpu.VMEM((len(joint) + 1, 1, lanes), f32),
            pltpu.VMEM((len(joint), joined, 1, lanes), f32),
            sems((3,)),
            sems((rounds, 2, 2, 2)),
            sems((rounds, 2, 2, 2)),
            sems((rounds, 2, 2)),
            sems((rounds, 2, 2)),
            sems((2, 2)),
            sems((2, 2)),
            sems((len(single), most)),
            sems((len(single), most)),
            sems((len(joint), joined)),
            sems((len(joint), joined)),
            sems((len(joint), joined)),
            sems((len(joint), joined)),
        ],
        compiler_params=pltpu.CompilerParams(collective_id=0, has_side_effects=True),
        name="powers",
    )(coefficients, earlier, start, shifts)
    new = pltpu.with_memory_space_constraint(new, pltpu.VMEM)
    small = pltpu.with_memory_space_constraint(small, pltpu.VMEM)
    new, proj, tri = pl.pallas_call(
        functools.partial(hand_over, rows),
        out_shape=(
            jax.ShapeDtypeStruct(new.shape, f32),
            jax.ShapeDtypeStruct((block, count), f32),
            jax.ShapeDtypeStruct((block, block), f32),
        ),
        in_specs=[vmem, vmem],
        out_specs=(anywhere, vmem, vmem),
        scratch_shapes=[sems((1,))],
        name="hand_over",
    )(new, small)
    return jnp.transpose(new, (0, 1, 3, 2, 4)), proj.T, tri


def solution(mesh):
    sizes = (("slab", mesh.shape["slab"]), ("sub", mesh.shape["sub"]))
    placed = (
        P(None, None, None, "slab", "sub", None),
        P(None, None, "slab", "sub", None),
        P(None, "slab", "sub", None),
        P(),
    )
    return jax.shard_map(
        functools.partial(body, sizes),
        mesh=mesh,
        in_specs=placed,
        out_specs=(P(None, None, "slab", "sub", None), P(), P()),
        check_vma=False,
    )
```

time: 35.5 us -> 28.9 us (0.81)
  Pallas kernels: 34.7 us -> 28.1 us
    pallas_call x1, Pallas kernels: 32.9 us -> 26.7 us  [body(): pl.pallas_call(functools.partial(kernel, sizes), out_shape=(pltpu.VMEM((b...]
    pallas_call x1, Pallas kernels: 1.81 us -> 1.37 us  [body(): pl.pallas_call(functools.partial(hand_over, rows), out_shape=(jax.ShapeDt...]
where the time goes in v1:
time: 28.9 us; the launch traced here: 28.7 us
  Pallas kernels  28.1 us (97%)
  between operations  0.64 us (2%)
    pallas_call x1, Pallas kernels, body(): pl.pallas_call(functools.partial(kernel, sizes), out_shape=(pltpu.VMEM((b...  26.7 us
    pallas_call x1, Pallas kernels, body(): pl.pallas_call(functools.partial(hand_over, rows), out_shape=(jax.ShapeDt...  1.37 us

profile of v1, /device:TPU:0, one launch (start us, length us, event | category | flops | bytes accessed | tf_op | source)
XLA Modules:
  0.0 28.7 jit_solution(8329385183394822133)
XLA Ops:
  0.6 26.7 %powers.1 = (f32[6,6,3,8,128]{4,3,2,1,0:T(8,128)S(1)}, f32[16,128]{1,0:T(8,128)S(1)}) custom-call(bf16[7,6,6,3,8,128]{5,4,3,2,1,0:T(8,128)(2,1)} %bitcast.6, f32[30,6,3,8,128]{4,3,2,1,0:T(8,128)} %bitcast.5, f32[6,3,8,128]{3,2,1,0:T(8,128)} %bitcast.7, f32[5]{0:T(128)} %shifts_ref.1), custom_call_target="tpu_custom_call" | custom-call | tf_op jit(solution)/shard_map/powers/pallas_call | solution.py:725
  27.3 1.4 %hand_over.1 = (f32[6,6,3,8,128]{4,3,2,1,0:T(8,128)}, f32[6,30]{1,0:T(8,128)}, f32[6,6]{1,0:T(8,128)}) custom-call(f32[6,6,3,8,128]{4,3,2,1,0:T(8,128)S(1)} %get-tuple-element.8.new_in, f32[16,128]{1,0:T(8,128)S(1)} %get-tuple-element.9.small), custom_call_target="tpu_custom_call" | custom-call | tf_op jit(solution)/shard_map/hand_over/pallas_call | solution.py:782

commit v2 on v1

--- a/solution.py
+++ b/solution.py
@@ -10,6 +10,7 @@
 MESH = pl.DeviceIdType.MESH
 LANES = 128
 ROWS = 8
+REACH = (2, 1)
 
 
 def dot(a, b, nt=False):
@@ -89,6 +90,13 @@
     return found
 
 
+def levels_of(extent):
+    levels = 0
+    while any(reach << levels < n - 1 for reach, n in zip(REACH, extent)):
+        levels += 1
+    return levels
+
+
 def members(stage):
     return stage[0][1] * stage[1][1]
 
@@ -117,13 +125,13 @@
 
 
 def kernel(
-    sizes, coef_hbm, early_hbm, start_hbm, shifts_ref, new_ref, small_ref,
+    sizes, coef_hbm, early_hbm, start_hbm, shifts_hbm, new_ref, proj_ref, tri_ref,
     coef_in, coef, edge_coef, gx_in, gz_send, gz_in, gz, allv, pieces, part, acc_ref,
     halo_x, halo_z, send_z, send_c, halo_c, pre_x, pre_z, ghost_x, ghost_z,
-    ee, sums_ref, late_ref,
+    ee, ee_cross, sums_ref, late_ref, small_ref,
     mine_ee, gathered_ee, mine_b, gathered_b, mine_f, gathered_f,
     in_sem, face_send, face_recv, corner_send, corner_recv, g_send, g_recv,
-    ee_send, ee_recv, b_send, b_recv, f_send, f_recv,
+    ee_send, ee_recv, b_send, b_recv, f_send, f_recv, ready, shifts_ref,
 ):
     depth = shifts_ref.shape[0]
     earlier, comp, width = early_hbm.shape[:3]
@@ -131,7 +139,7 @@
     count = comp * width * ROWS * LANES * sizes[0][1] * sizes[1][1]
     half = LANES // 2
     rounds = steps_of(depth)
-    single = stages_of(sizes)
+    single = stages_of(sizes)[::-1]
     joint = joint_stages_of(sizes)
     place = [lax.axis_index(axis) for axis, _ in sizes]
     extent = [n for _, n in sizes]
@@ -142,15 +150,11 @@
     copy_start = pltpu.make_async_copy(start_hbm, allv.at[earlier], in_sem.at[0])
     copy_coef = pltpu.make_async_copy(coef_hbm, coef_in, in_sem.at[1])
     copy_early = pltpu.make_async_copy(early_hbm, allv.at[pl.ds(0, earlier)], in_sem.at[2])
+    copy_shifts = pltpu.make_async_copy(shifts_hbm, shifts_ref, in_sem.at[3])
     copy_start.start()
+    copy_shifts.start()
     copy_coef.start()
     copy_early.start()
-
-    halo_x[...] = jnp.zeros_like(halo_x)
-    halo_z[...] = jnp.zeros_like(halo_z)
-    halo_c[...] = jnp.zeros_like(halo_c)
-    gx_in[...] = jnp.zeros_like(gx_in)
-    gz_in[...] = jnp.zeros_like(gz_in)
 
     def there(kind, side, sending):
         upward = (side == 0) == sending
@@ -174,30 +178,67 @@
         flat = stage[1][1]
         return mine_at[0] * flat + mine_at[1], peer_at[0] * flat + peer_at[1], target
 
+    levels = levels_of(extent)
+
+    def around(reach, unit, act):
+        for dz in range(-reach[0], reach[0] + 1):
+            for dx in range(-reach[1], reach[1] + 1):
+                far = (unit[0] * dz, unit[1] * dx)
+                if far != (0, 0):
+                    a, b = place[0] + far[0], place[1] + far[1]
+
+                    @pl.when((a >= 0) & (a < extent[0]) & (b >= 0) & (b < extent[1]))
+                    def _():
+                        act(at_peer(*far))
+
+    def signal(sem):
+        return lambda where: pl.semaphore_signal(
+            sem, inc=1, device_id=where, device_id_type=MESH
+        )
+
+    def wait_around(sem, reach, unit):
+        total = 1
+        for axis in (0, 1):
+            seen = 1
+            for d in range(1, reach[axis] + 1):
+                far = d * unit[axis]
+                seen = seen + jnp.where(place[axis] >= far, 1, 0)
+                seen = seen + jnp.where(place[axis] + far < extent[axis], 1, 0)
+            total = total * seen
+        pl.semaphore_wait(sem, total - 1)
+
+    def greet(level):
+        if 0 < level <= levels:
+            unit = tuple(x << (level - 1) for x in REACH)
+            wait_around(ready.at[level - 1], (1, 1), unit)
+        if level < levels:
+            unit = tuple(x << level for x in REACH)
+            around((1, 1), unit, signal(ready.at[level]))
+
     barrier = pltpu.get_barrier_semaphore()
-    expected = 0
-    for stage in single + joint:
-        for offset in offsets_of(stage):
-            _, _, target = peer(stage, offset)
-            pl.semaphore_signal(barrier, inc=1, device_id=target, device_id_type=MESH)
-            expected += 1
-    around = [(dz, dx) for dz in (-1, 0, 1) for dx in (-1, 0, 1) if dz or dx]
-    beyond = around if len(joint) > 1 else []
-
-    def exists(dz, dx):
-        a = place[0] + dz
-        b = place[1] + dx
-        return (a >= 0) & (a < extent[0]) & (b >= 0) & (b < extent[1])
-
-    for dz, dx in beyond:
-        @pl.when(exists(dz, dx))
-        def _():
-            pl.semaphore_signal(barrier, inc=1, device_id=at_peer(dz, dx), device_id_type=MESH)
+    around(REACH, (1, 1), signal(barrier))
+
+    for kind in (0, 1):
+        for side in (0, 1):
+            @pl.when(jnp.logical_not(there(kind, side, False)))
+            def _():
+                halo, coupling = (halo_z, gz_in) if kind == 0 else (halo_x, gx_in)
+                for r in range(len(rounds)):
+                    for what in (0, 1):
+                        halo[r, what, side] = jnp.zeros_like(halo[r, what, side])
+                coupling[side] = jnp.zeros_like(coupling[side])
+    for sz in (0, 1):
+        for sx in (0, 1):
+            @pl.when(jnp.logical_not(there(0, sz, False) & there(1, sx, False)))
+            def _():
+                for r in range(len(rounds)):
+                    halo_c[r, sz, sx] = jnp.zeros_like(halo_c[r, sz, sx])
 
     send_z[...] = jnp.zeros_like(send_z)
     send_c[...] = jnp.zeros_like(send_c)
     edge_coef[...] = jnp.zeros_like(edge_coef)
     ee[...] = jnp.zeros_like(ee)
+    ee_cross[...] = jnp.zeros_like(ee_cross)
     sums_ref[...] = jnp.zeros_like(sums_ref)
     late_ref[...] = jnp.zeros_like(late_ref)
 
@@ -211,15 +252,15 @@
         dz, dx = (toward(side), 0) if kind == 0 else (0, toward(side))
         return pltpu.make_async_remote_copy(
             src_ref=src, dst_ref=dst,
-            send_sem=face_send.at[r, what, kind, side],
-            recv_sem=face_recv.at[r, what, kind, side],
+            send_sem=face_send.at[what, kind, side],
+            recv_sem=face_recv.at[r % 2, what, kind, side],
             device_id=at_peer(dz, dx), device_id_type=MESH,
         )
 
     def corner_copy(r, sz, sx):
         return pltpu.make_async_remote_copy(
             src_ref=send_c.at[r, sz, sx], dst_ref=halo_c.at[r, sz, sx],
-            send_sem=corner_send.at[r, sz, sx], recv_sem=corner_recv.at[r, sz, sx],
+            send_sem=corner_send.at[sz, sx], recv_sem=corner_recv.at[r % 2, sz, sx],
             device_id=at_peer(toward(sz), toward(sx)), device_id_type=MESH,
         )
 
@@ -339,17 +380,43 @@
     def as_line(value):
         return jnp.sum(value.T, axis=0, keepdims=True)
 
+    def times(a, b):
+        return lax.dot_general(
+            a, b, (((1,), (1,)), ((), ())), preferred_element_type=jnp.float32
+        )
+
     def self_products(c):
         parts = split(side_by_side(allv[pl.ds(0, earlier), c]))
         for at, piece in enumerate(parts):
             pieces[at, c] = piece
-        ee[...] += dot_pieces(parts, [parts[0], parts[1], parts[2]], nt=True)
+        one = times(parts[0], parts[0])
+        two = times(jnp.concatenate(parts[:2], axis=0), parts[1])
+        three = times(parts[0], parts[2])
+        span = earlier * ROWS
+        ee[...] += one + two[span:]
+        ee_cross[...] += two[:span] + three
+
+    def gather_self(value):
+        span = earlier * ROWS
+        rows = jnp.sum(diagonal(value).reshape(earlier, ROWS, span), axis=1)
+        own = onehot((span, LANES), lambda r, q: (r >> 3) == q).astype(jnp.bfloat16)
+        found = None
+        for piece in split(rows)[::-1]:
+            some = lax.dot_general(
+                piece, own, (((1,), (0,)), ((), ())), preferred_element_type=jnp.float32
+            )
+            found = some if found is None else found + some
+        return jnp.concatenate(
+            [found, jnp.zeros((LANES - earlier, LANES), jnp.float32)], axis=0
+        )
 
     def self_finish():
-        span = earlier * ROWS
-        wide = dot(diagonal(ee[...]), onehot((span, LANES), lambda r, q: (r >> 3) == (q & 31)))
-        wide = jnp.where((iota(wide.shape, 0) >> 6) == (iota(wide.shape, 1) >> 5), wide, 0.0)
-        mine_ee[0] = dot(onehot((ROWS, span), lambda r, q: ((q >> 3) & 7) == r), wide)
+        cross = gather_self(ee_cross[...])
+        whole = gather_self(ee[...])[:32] + (cross + cross.T)[:32]
+        packed = whole[:ROWS]
+        for g in range(1, 4):
+            packed = packed + pltpu.roll(whole[ROWS * g:ROWS * (g + 1)], 32 * g, 1)
+        mine_ee[0] = packed
 
     exchanges = {
         "ee": (single, mine_ee, gathered_ee, ee_send, ee_recv),
@@ -360,39 +427,35 @@
     def begin(name, at):
         stages, own, slots, send_sem, recv_sem = exchanges[name]
         for offset in offsets_of(stages[at]):
-            here, other, target = peer(stages[at], offset)
+            here, _, target = peer(stages[at], offset)
             pltpu.make_async_remote_copy(
                 src_ref=own.at[at], dst_ref=slots.at[at, here],
-                send_sem=send_sem.at[at, other], recv_sem=recv_sem.at[at, here],
+                send_sem=send_sem.at[at], recv_sem=recv_sem.at[at],
                 device_id=target, device_id_type=MESH,
             ).start()
 
+    def all_of(name, at):
+        stages, own, slots, send_sem, recv_sem = exchanges[name]
+        others = slots.at[at, pl.ds(0, members(stages[at]) - 1)]
+        _, _, target = peer(stages[at], offsets_of(stages[at])[0])
+        return pltpu.make_async_remote_copy(
+            src_ref=others, dst_ref=others, send_sem=send_sem.at[at], recv_sem=recv_sem.at[at],
+            device_id=target, device_id_type=MESH,
+        )
+
     def finish(name, at):
-        stages, own, slots, send_sem, recv_sem = exchanges[name]
+        stages, own, slots, _, _ = exchanges[name]
         here, _, _ = peer(stages[at], (0, 0))
         slots[at, here] = own[at]
-        for offset in offsets_of(stages[at]):
-            _, other, target = peer(stages[at], offset)
-            pltpu.make_async_remote_copy(
-                src_ref=own.at[at], dst_ref=slots.at[at, other],
-                send_sem=send_sem.at[at, other], recv_sem=recv_sem.at[at, other],
-                device_id=target, device_id_type=MESH,
-            ).wait_recv()
+        all_of(name, at).wait_recv()
         whole = slots[at, 0]
         for other in range(1, members(stages[at])):
             whole = whole + slots[at, other]
         own[at + 1] = whole
 
     def drain(name):
-        stages, own, slots, send_sem, recv_sem = exchanges[name]
-        for at, stage in enumerate(stages):
-            for offset in offsets_of(stage):
-                here, other, target = peer(stage, offset)
-                pltpu.make_async_remote_copy(
-                    src_ref=own.at[at], dst_ref=slots.at[at, here],
-                    send_sem=send_sem.at[at, other], recv_sem=recv_sem.at[at, here],
-                    device_id=target, device_id_type=MESH,
-                ).wait_send()
+        for at in range(len(exchanges[name][0])):
+            all_of(name, at).wait_send()
 
     def whole_exchange(name, first):
         stages = exchanges[name][0]
@@ -481,228 +544,280 @@
                     )
                 ghost_x[side, c] = value
 
-    copy_start.wait()
-    for dz, dx in beyond:
-        @pl.when(exists(dz, dx))
-        def _():
-            pl.semaphore_wait(barrier, 1)
-    pl.semaphore_wait(barrier, expected)
+    with jax.named_scope("start"):
+        copy_start.wait()
+        wait_around(barrier, REACH, (1, 1))
+        greet(0)
 
     step = 0
     comps = list(range(comp))
     paired = [r for r, size in enumerate(rounds) if size == 2]
-    per_round = -(-comp // max(1, len(rounds) - 1))
-    done = 0
-    ee_begun = False
+    before = max(1, len(rounds) - 1)
+    share = [2 * comp // (before + 1)] + [comp // (before + 1)] * (before - 1)
+    share[-1] += comp - sum(share)
+    share += [0] * (len(rounds) - len(share))
+    greeted, ee_at, self_at, done = 1, None, 0, 0
+
+    def self_some(low, high):
+        @pl.loop(low, high)
+        def _(c):
+            self_products(c)
+
     for r, size in enumerate(rounds):
-        send_faces(r, step)
+        with jax.named_scope(f"send{r}"):
+            if r:
+                each_face(
+                    True, (0, 1), lambda kind, side: face_copy(r - 1, 0, 0, kind, side).wait_send()
+                )
+            send_faces(r, step)
         if r == 0:
-            copy_coef.wait()
-            load_coefficients()
-            each_face(True, (0, 1), lambda kind, side: g_copy(kind, side).start())
-        if size == 2 and r == paired[0]:
-            take_couplings()
+            with jax.named_scope("load"):
+                copy_coef.wait()
+                load_coefficients()
+                each_face(True, (0, 1), lambda kind, side: g_copy(kind, side).start())
+                copy_shifts.wait()
+        with jax.named_scope(f"neigh{r}"):
+            if size == 2 and r == paired[0]:
+                take_couplings()
+            if size == 2:
+                if r > paired[0]:
+                    each_corner(True, lambda sz, sx: corner_copy(r - 1, sz, sx).wait_send())
+                complete_neighbours(r, step)
+        with jax.named_scope(f"local{r}"):
+            part[r] = apply_local(step)
+        with jax.named_scope(f"part{r}"):
+            if size == 2:
+                pack(r, 1, lambda e, x: part.at[r, e, x])
+                if r > paired[0]:
+                    each_face(
+                        True, (0, 1),
+                        lambda kind, side: face_copy(r - 1, 0, 1, kind, side).wait_send(),
+                    )
+                each_face(True, (0, 1), lambda kind, side: face_copy(r, step, 1, kind, side).start())
+            if r == 0:
+                copy_early.wait()
+        with jax.named_scope(f"cross{r}"):
+            for k in range(done, min(step + 1, late)):
+                cross_products(k, sums_ref.at[k // 2], (k % 2) * half)
+                done = k + 1
+        with jax.named_scope(f"self{r}"):
+            if share[r]:
+                middle = self_at + share[r] // 2
+                if r == 0:
+                    self_some(self_at, middle)
+                    greet(greeted)
+                    greeted += 1
+                    self_some(middle, self_at + share[r])
+                else:
+                    if greeted <= levels:
+                        greet(greeted)
+                        greeted += 1
+                    self_some(self_at, self_at + share[r])
+                self_at += share[r]
+        with jax.named_scope(f"ee{r}"):
+            if share[r] and self_at == comp:
+                self_finish()
+                while greeted <= levels:
+                    greet(greeted)
+                    greeted += 1
+                begin("ee", 0)
+                ee_at = 0
+            elif ee_at == 0 and len(single) > 1:
+                finish("ee", 0)
+                begin("ee", 1)
+                ee_at = 1
+            if done == late and r == len(rounds) - 1:
+                for q in range(lines):
+                    mine_b[0, q] = as_line(sums_ref[q])
+                begin("b", 0)
+        with jax.named_scope(f"faces{r}"):
+            take_faces(r, step, lambda x, r=r: part[r, :, x])
         if size == 2:
-            complete_neighbours(r, step)
-        part[r] = apply_local(step)
-        if size == 2:
-            pack(r, 1, lambda e, x: part.at[r, e, x])
-            each_face(True, (0, 1), lambda kind, side: face_copy(r, step, 1, kind, side).start())
-        if r == 0:
-            copy_early.wait()
-        for k in range(done, min(step + 1, late)):
-            cross_products(k, sums_ref.at[k // 2], (k % 2) * half)
-            done = k + 1
-        if done == late and r == len(rounds) - 1:
-            for q in range(lines):
-                mine_b[0, q] = as_line(sums_ref[q])
-            begin("b", 0)
-        todo, comps = comps[:per_round], comps[per_round:]
-        if todo:
-            @pl.loop(todo[0], todo[-1] + 1)
-            def _(c):
-                self_products(c)
-        if ee_begun:
-            finish("ee", 0)
-            if len(single) > 1:
-                begin("ee", 1)
-            ee_begun = False
-        if todo and not comps:
-            self_finish()
-            begin("ee", 0)
-            ee_begun = len(rounds) - 1 > r
-        take_faces(r, step, lambda x, r=r: part[r, :, x])
-        if size == 2:
-            if r == len(rounds) - 1:
-                cross_products(step + 1, late_ref, 0)
-            acc_ref[...] = apply_local(step + 1)
-            take_ghosts(r, step)
-            sides = add_x(lambda x: acc_ref[:, x], lambda side, e: ghost_x[side, e])
-            edge = add_z(lambda e: ghost_z[e])
-            store_step(step + 2, lambda x: acc_ref[:, x], sides, edge)
+            with jax.named_scope(f"late{r}"):
+                if r == len(rounds) - 1:
+                    cross_products(step + 1, late_ref, 0)
+            with jax.named_scope(f"second{r}"):
+                acc_ref[...] = apply_local(step + 1)
+            with jax.named_scope(f"ghost{r}"):
+                take_ghosts(r, step)
+            with jax.named_scope(f"store{r}"):
+                sides = add_x(lambda x: acc_ref[:, x], lambda side, e: ghost_x[side, e])
+                edge = add_z(lambda e: ghost_z[e])
+                store_step(step + 2, lambda x: acc_ref[:, x], sides, edge)
         step += size
 
-    cross_products(depth, late_ref, half)
-    mine_f[0] = as_line(late_ref[...])
-    begin("f", 0)
-
-    ee_from = 1 if len(single) > 1 else 0
-    for at in range(ee_from, len(single)):
-        if at > ee_from:
-            begin("ee", at)
-        finish("ee", at)
-    packed = mine_ee[len(single)] * (1.0 / count)
-    early = whole_exchange("b", True)
-
-    row, lane = iota((ROWS, LANES), 0), iota((ROWS, LANES), 1)
-    found = jnp.concatenate(
-        [
-            early[k // 2] if k % 2 == 0 else pltpu.roll(early[k // 2], half, 1)
+    with jax.named_scope("last"):
+        cross_products(depth, late_ref, half)
+        mine_f[0] = as_line(late_ref[...])
+        begin("f", 0)
+
+    with jax.named_scope("eewait"):
+        for at in range(ee_at, len(single)):
+            if at > ee_at:
+                begin("ee", at)
+            finish("ee", at)
+        packed = mine_ee[len(single)] * (1.0 / count)
+    with jax.named_scope("bwait"):
+        early = whole_exchange("b", True)
+
+    with jax.named_scope("algebra"):
+        row, lane = iota((ROWS, LANES), 0), iota((ROWS, LANES), 1)
+        found = jnp.concatenate(
+            [
+                early[k // 2] if k % 2 == 0 else pltpu.roll(early[k // 2], half, 1)
+                for k in range(late)
+            ] + [jnp.zeros((ROWS - late, LANES), jnp.float32)], axis=0
+        )
+        proj_t = jnp.where(lane < earlier, found, 0.0)
+        known = jnp.where(lane < earlier + row, found, 0.0)
+        pick = onehot((ROWS, LANES), lambda r, q: q == r + earlier)
+        gram = jnp.where(lane <= earlier + row, found, 0.0)
+        gram = pltpu.roll(gram, LANES - earlier, 1)[:, :ROWS]
+        square = jnp.concatenate(
+            [packed] + [pltpu.roll(packed, LANES - 32 * g, 1) for g in range(1, 4)], axis=0
+        )
+        sr, sl = iota(square.shape, 0), iota(square.shape, 1)
+        inside = (sl < earlier) & (sr < earlier)
+        square = jnp.where(inside, square - jnp.where(sr == sl, 2.0, 0.0), 0.0)
+        moved = dot(proj_t[:, :32], square) + pick
+        gram = gram + dot(moved, known, nt=True)
+
+        upper = gram
+        inverse = onehot((ROWS, ROWS), lambda r, q: (r == q) & (r < late))
+        r8 = iota((ROWS, ROWS), 0)
+        q8 = iota((ROWS, ROWS), 1)
+        for p in range(late):
+            pivot = upper[p:p + 1, p:p + 1]
+            scale = inverse_root(pivot)
+            column = upper[:, p:p + 1] * scale
+            row_u, row_i = upper[p:p + 1, :] * scale, inverse[p:p + 1, :] * scale
+            upper = jnp.where(r8 == p, row_u, jnp.where(r8 > p, upper - column * row_u, upper))
+            inverse = jnp.where(r8 == p, row_i, jnp.where(r8 > p, inverse - column * row_i, inverse))
+        onto = dot(inverse, moved)
+
+        mix = dot(inverse, pick - proj_t)
+        tall = dot(onehot((late * ROWS, ROWS), lambda r, q: (r >> 3) == q), mix)
+        span = earlier * ROWS
+        mix = split(diagonal(dot(tall, onehot((LANES, span), lambda r, q: (q >> 3) == r))))
+        weights = [
+            [
+                jnp.broadcast_to(
+                    tall[k * ROWS:(k + 1) * ROWS, earlier + i:earlier + i + 1], (ROWS, LANES)
+                )
+                for i in range(k + 1)
+            ]
             for k in range(late)
-        ] + [jnp.zeros((ROWS - late, LANES), jnp.float32)], axis=0
-    )
-    proj_t = jnp.where(lane < earlier, found, 0.0)
-    known = jnp.where(lane < earlier + row, found, 0.0)
-    pick = onehot((ROWS, LANES), lambda r, q: q == r + earlier)
-    gram = jnp.where(lane <= earlier + row, found, 0.0)
-    gram = pltpu.roll(gram, LANES - earlier, 1)[:, :ROWS]
-    square = jnp.concatenate(
-        [packed] + [pltpu.roll(packed, LANES - 32 * g, 1) for g in range(1, 4)], axis=0
-    )
-    sr, sl = iota(square.shape, 0), iota(square.shape, 1)
-    inside = (sl < earlier) & (sr < earlier)
-    square = jnp.where(inside, square - jnp.where(sr == sl, 2.0, 0.0), 0.0)
-    moved = dot(proj_t[:, :32], square) + pick
-    gram = gram + dot(moved, known, nt=True)
-
-    upper = gram
-    inverse = onehot((ROWS, ROWS), lambda r, q: (r == q) & (r < late))
-    r8 = iota((ROWS, ROWS), 0)
-    q8 = iota((ROWS, ROWS), 1)
-    for p in range(late):
-        pivot = upper[p:p + 1, p:p + 1]
-        scale = inverse_root(pivot)
-        column = upper[:, p:p + 1] * scale
-        row_u, row_i = upper[p:p + 1, :] * scale, inverse[p:p + 1, :] * scale
-        upper = jnp.where(r8 == p, row_u, jnp.where(r8 > p, upper - column * row_u, upper))
-        inverse = jnp.where(r8 == p, row_i, jnp.where(r8 > p, inverse - column * row_i, inverse))
-    onto = dot(inverse, moved)
-
-    mix = dot(inverse, pick - proj_t)
-    tall = dot(onehot((late * ROWS, ROWS), lambda r, q: (r >> 3) == q), mix)
-    span = earlier * ROWS
-    mix = split(diagonal(dot(tall, onehot((LANES, span), lambda r, q: (q >> 3) == r))))
-    weights = [
-        [
-            jnp.broadcast_to(
-                tall[k * ROWS:(k + 1) * ROWS, earlier + i:earlier + i + 1], (ROWS, LANES)
+        ]
+    with jax.named_scope("out"):
+        for c in range(comp):
+            out = dot_pieces(mix, [pieces[at, c] for at in range(3)])
+            for x in range(width):
+                for k in range(late):
+                    value = out[k * ROWS:(k + 1) * ROWS, LANES * x:LANES * (x + 1)]
+                    for i in range(k + 1):
+                        value = value + weights[k][i] * allv[earlier + i, c, x]
+                    new_ref[k, c, x] = value
+        small_ref[0:ROWS, :] = proj_t
+        small_ref[ROWS:2 * ROWS, :] = jnp.zeros((ROWS, LANES), jnp.float32)
+        small_ref[ROWS:2 * ROWS, 0:ROWS] = jnp.where((q8 >= r8) & (r8 < late), upper, 0.0)
+
+    with jax.named_scope("sent"):
+        r = len(rounds) - 1
+        for what in range(2 if paired else 1):
+            at = paired[-1] if what else r
+            each_face(
+                True, (0, 1), lambda kind, side: face_copy(at, 0, what, kind, side).wait_send()
             )
-            for i in range(k + 1)
-        ]
-        for k in range(late)
-    ]
-    for c in range(comp):
-        out = dot_pieces(mix, [pieces[at, c] for at in range(3)])
-        for x in range(width):
-            for k in range(late):
-                value = out[k * ROWS:(k + 1) * ROWS, LANES * x:LANES * (x + 1)]
-                for i in range(k + 1):
-                    value = value + weights[k][i] * allv[earlier + i, c, x]
-                new_ref[k, c, x] = value
-    small_ref[0:ROWS, :] = proj_t
-    small_ref[ROWS:2 * ROWS, :] = jnp.zeros((ROWS, LANES), jnp.float32)
-    small_ref[ROWS:2 * ROWS, 0:ROWS] = jnp.where((q8 >= r8) & (r8 < late), upper, 0.0)
-
-    final = whole_exchange("f", True)
-    ys = [final, pltpu.roll(final, half, 1)][2 - (block - late):]
-    spread = [jnp.broadcast_to(y, (ROWS, LANES)) for y in ys]
-    tiles = -(-(earlier + block) // ROWS)
-    columns = []
-    for y in spread:
-        col = [
-            lane_sums(jnp.where(lane == row + ROWS * t, y, 0.0)) for t in range(tiles)
-        ]
-        img = [
-            lane_sums(square[ROWS * t:ROWS * (t + 1)] * y) for t in range(square.shape[0] // ROWS)
-        ]
-        columns.append((col, img, lane_sums(onto * y)))
-    wide = lambda value: jnp.broadcast_to(value, (ROWS, LANES))
-
-    def inner(a, b):
-        (col_a, _, r_a), (col_b, img_b, r_b) = columns[a], columns[b]
-        total = -(r_a * r_b)
-        for t in range(len(img_b)):
-            total = total + jnp.where(row[:, :1] + ROWS * t < earlier, col_a[t] * img_b[t], 0.0)
-        for t in range(tiles):
-            total = total + jnp.where(row[:, :1] + ROWS * t == earlier + late + a, col_b[t], 0.0)
-        return sublane_sums(wide(total))
-
-    fresh = block - late
-    scales, ratios, lines_out = [], {}, []
-    for b in range(fresh):
-        value = inner(b, b)
-        for a in range(b):
-            cross = inner(a, b)
-            ratios[a, b] = cross * scales[a]
-            value = value - ratios[a, b] * ratios[a, b]
-        scales.append(inverse_root(value))
-        ratios[b, b] = value * scales[b]
-    triangle = small_ref[ROWS:2 * ROWS, :]
-    proj_rows = small_ref[0:ROWS, :]
-    for b in range(fresh):
-        k = late + b
-        triangle = triangle + jnp.where(lane == k, wide(columns[b][2]), 0.0)
-        for a in range(b + 1):
-            triangle = triangle + jnp.where((lane == k) & (row == late + a), ratios[a, b], 0.0)
-        proj_rows = jnp.where((row == k) & (lane < earlier), spread[b], proj_rows)
-    small_ref[ROWS:2 * ROWS, :] = triangle
-    small_ref[0:ROWS, :] = proj_rows
-    for b in range(fresh):
-        for t in range(tiles):
-            late_ref[b * half + ROWS * t:b * half + ROWS * (t + 1), :] = wide(columns[b][0][t])
-        late_ref[b * half + ROWS * tiles:b * half + ROWS * (tiles + 1), :] = wide(columns[b][2])
-
-    for c in range(comp):
-        totals = [allv[earlier + late + b, c] for b in range(fresh)]
-        for j in range(earlier):
-            v = allv[j, c]
+        if paired:
+            each_corner(True, lambda sz, sx: corner_copy(paired[-1], sz, sx).wait_send())
+        each_face(True, (0, 1), lambda kind, side: g_copy(kind, side).wait_send())
+        drain("ee")
+        drain("b")
+    with jax.named_scope("fwait"):
+        final = whole_exchange("f", True)
+    with jax.named_scope("columns"):
+        ys = [final, pltpu.roll(final, half, 1)][2 - (block - late):]
+        spread = [jnp.broadcast_to(y, (ROWS, LANES)) for y in ys]
+        tiles = -(-(earlier + block) // ROWS)
+        columns = []
+        for y in spread:
+            col = [
+                lane_sums(jnp.where(lane == row + ROWS * t, y, 0.0)) for t in range(tiles)
+            ]
+            img = [
+                lane_sums(square[ROWS * t:ROWS * (t + 1)] * y) for t in range(square.shape[0] // ROWS)
+            ]
+            columns.append((col, img, lane_sums(onto * y)))
+        wide = lambda value: jnp.broadcast_to(value, (ROWS, LANES))
+
+        def inner(a, b):
+            (col_a, _, r_a), (col_b, img_b, r_b) = columns[a], columns[b]
+            total = -(r_a * r_b)
+            for t in range(len(img_b)):
+                total = total + jnp.where(row[:, :1] + ROWS * t < earlier, col_a[t] * img_b[t], 0.0)
+            for t in range(tiles):
+                total = total + jnp.where(row[:, :1] + ROWS * t == earlier + late + a, col_b[t], 0.0)
+            return sublane_sums(wide(total))
+
+        fresh = block - late
+        scales, ratios, lines_out = [], {}, []
+        for b in range(fresh):
+            value = inner(b, b)
+            for a in range(b):
+                cross = inner(a, b)
+                ratios[a, b] = cross * scales[a]
+                value = value - ratios[a, b] * ratios[a, b]
+            scales.append(inverse_root(value))
+            ratios[b, b] = value * scales[b]
+        triangle = small_ref[ROWS:2 * ROWS, :]
+        proj_rows = small_ref[0:ROWS, :]
+        for b in range(fresh):
+            k = late + b
+            triangle = triangle + jnp.where(lane == k, wide(columns[b][2]), 0.0)
+            for a in range(b + 1):
+                triangle = triangle + jnp.where((lane == k) & (row == late + a), ratios[a, b], 0.0)
+            proj_rows = jnp.where((row == k) & (lane < earlier), spread[b], proj_rows)
+        small_ref[ROWS:2 * ROWS, :] = triangle
+        small_ref[0:ROWS, :] = proj_rows
+        for b in range(fresh):
+            for t in range(tiles):
+                late_ref[b * half + ROWS * t:b * half + ROWS * (t + 1), :] = wide(columns[b][0][t])
+            late_ref[b * half + ROWS * tiles:b * half + ROWS * (tiles + 1), :] = wide(columns[b][2])
+
+    with jax.named_scope("tail"):
+        for c in range(comp):
+            totals = [allv[earlier + late + b, c] for b in range(fresh)]
+            for j in range(earlier):
+                v = allv[j, c]
+                for b in range(fresh):
+                    at = b * half + j
+                    totals[b] = totals[b] - late_ref[at:at + 1, :] * v
+            for i in range(late):
+                v = new_ref[i, c]
+                for b in range(fresh):
+                    at = b * half + ROWS * tiles + i
+                    totals[b] = totals[b] - late_ref[at:at + 1, :] * v
+            outs = []
             for b in range(fresh):
-                at = b * half + j
-                totals[b] = totals[b] - late_ref[at:at + 1, :] * v
-        for i in range(late):
-            v = new_ref[i, c]
-            for b in range(fresh):
-                at = b * half + ROWS * tiles + i
-                totals[b] = totals[b] - late_ref[at:at + 1, :] * v
-        outs = []
-        for b in range(fresh):
-            value = totals[b]
-            for a in range(b):
-                value = value - ratios[a, b] * outs[a]
-            outs.append(value * scales[b])
-            new_ref[late + b, c] = outs[b]
-
-    step = 0
-    for r, size in enumerate(rounds):
-        for what in range(size):
-            each_face(
-                True, (0, 1),
-                lambda kind, side: face_copy(r, step, what, kind, side).wait_send(),
-            )
-        if size == 2:
-            each_corner(True, lambda sz, sx: corner_copy(r, sz, sx).wait_send())
-        step += size
-    each_face(True, (0, 1), lambda kind, side: g_copy(kind, side).wait_send())
-    for name in exchanges:
-        drain(name)
-
-
-def hand_over(rows, new_in, small, new_out, proj_out, tri_out, sem):
-    copy = pltpu.make_async_copy(new_in, new_out, sem.at[0])
-    copy.start()
-    proj_out[...] = small[: proj_out.shape[0], : proj_out.shape[1]]
-    tri_out[...] = small[rows:rows + tri_out.shape[0], : tri_out.shape[1]]
-    copy.wait()
+                value = totals[b]
+                for a in range(b):
+                    value = value - ratios[a, b] * outs[a]
+                outs.append(value * scales[b])
+                new_ref[late + b, c] = outs[b]
+
+    with jax.named_scope("drain"):
+        drain("f")
+        proj_ref[...] = small_ref[:block, :earlier]
+        tri_ref[...] = small_ref[ROWS:ROWS + block, :block]
+
+
+def hand_over(new_in, proj_in, tri_in, new_out, proj_out, tri_out, sem):
+    pairs = ((new_in, new_out), (proj_in, proj_out), (tri_in, tri_out))
+    copies = [pltpu.make_async_copy(*pair, sem.at[at]) for at, pair in enumerate(pairs)]
+    for copy in copies:
+        copy.start()
+    for copy in copies:
+        copy.wait()
 
 
 def body(sizes, coefficients, earlier, start, shifts):
@@ -718,18 +833,20 @@
     single, joint = stages_of(sizes), joint_stages_of(sizes)
     most = max(members(stage) for stage in single)
     joined = max(members(stage) for stage in joint)
+    levels = max(1, levels_of([n for _, n in sizes]))
     f32, b16 = jnp.float32, jnp.bfloat16
     anywhere = pl.BlockSpec(memory_space=pl.ANY)
     vmem = pl.BlockSpec(memory_space=pltpu.VMEM)
     sems = pltpu.SemaphoreType.DMA
-    new, small = pl.pallas_call(
+    found = pl.pallas_call(
         functools.partial(kernel, sizes),
         out_shape=(
             pltpu.VMEM((block, comp, width, rows, lanes), f32),
-            pltpu.VMEM((2 * rows, lanes), f32),
+            pltpu.VMEM((block, count), f32),
+            pltpu.VMEM((block, block), f32),
         ),
-        in_specs=[anywhere, anywhere, anywhere, pl.BlockSpec(memory_space=pltpu.SMEM)],
-        out_specs=(vmem, vmem),
+        in_specs=[anywhere] * 4,
+        out_specs=(vmem, vmem, vmem),
         scratch_shapes=[
             pltpu.VMEM(coefficients.shape, coefficients.dtype),
             pltpu.VMEM(coefficients.shape, f32),
@@ -752,45 +869,44 @@
             pltpu.VMEM((2, comp, rows, lanes), f32),
             pltpu.VMEM((comp, rows, lanes), f32),
             pltpu.VMEM((count * rows, count * rows), f32),
+            pltpu.VMEM((count * rows, count * rows), f32),
             pltpu.VMEM((lines, lanes, lanes), f32),
             pltpu.VMEM((lanes, lanes), f32),
+            pltpu.VMEM((2 * rows, lanes), f32),
             pltpu.VMEM((len(single) + 1, rows, lanes), f32),
             pltpu.VMEM((len(single), most, rows, lanes), f32),
             pltpu.VMEM((len(joint) + 1, lines, 1, lanes), f32),
             pltpu.VMEM((len(joint), joined, lines, 1, lanes), f32),
             pltpu.VMEM((len(joint) + 1, 1, lanes), f32),
             pltpu.VMEM((len(joint), joined, 1, lanes), f32),
-            sems((3,)),
-            sems((rounds, 2, 2, 2)),
-            sems((rounds, 2, 2, 2)),
-            sems((rounds, 2, 2)),
-            sems((rounds, 2, 2)),
+            sems((4,)),
+            sems((2, 2, 2)),
+            sems((2, 2, 2, 2)),
+            sems((2, 2)),
+            sems((2, 2, 2)),
             sems((2, 2)),
             sems((2, 2)),
-            sems((len(single), most)),
-            sems((len(single), most)),
-            sems((len(joint), joined)),
-            sems((len(joint), joined)),
-            sems((len(joint), joined)),
-            sems((len(joint), joined)),
+            sems((len(single),)),
+            sems((len(single),)),
+            sems((len(joint),)),
+            sems((len(joint),)),
+            sems((len(joint),)),
+            sems((len(joint),)),
+            pltpu.SemaphoreType.REGULAR((levels,)),
+            pltpu.SMEM(shifts.shape, f32),
         ],
         compiler_params=pltpu.CompilerParams(collective_id=0, has_side_effects=True),
         name="powers",
     )(coefficients, earlier, start, shifts)
-    new = pltpu.with_memory_space_constraint(new, pltpu.VMEM)
-    small = pltpu.with_memory_space_constraint(small, pltpu.VMEM)
+    found = [pltpu.with_memory_space_constraint(value, pltpu.VMEM) for value in found]
     new, proj, tri = pl.pallas_call(
-        functools.partial(hand_over, rows),
-        out_shape=(
-            jax.ShapeDtypeStruct(new.shape, f32),
-            jax.ShapeDtypeStruct((block, count), f32),
-            jax.ShapeDtypeStruct((block, block), f32),
-        ),
-        in_specs=[vmem, vmem],
-        out_specs=(anywhere, vmem, vmem),
-        scratch_shapes=[sems((1,))],
+        hand_over,
+        out_shape=[jax.ShapeDtypeStruct(value.shape, f32) for value in found],
+        in_specs=[vmem] * 3,
+        out_specs=[anywhere] * 3,
+        scratch_shapes=[sems((3,))],
         name="hand_over",
-    )(new, small)
+    )(*found)
     return jnp.transpose(new, (0, 1, 3, 2, 4)), proj.T, tri
 
 

time: 28.9 us -> 23.8 us (0.82)
  Pallas kernels: 28.1 us -> 23.1 us
    pallas_call x1, Pallas kernels: 26.7 us -> 22.3 us  [body(): pl.pallas_call(functools.partial(kernel, sizes), out_shape=(pltpu.VMEM((b...]
    pallas_call x1, Pallas kernels: 1.37 us -> 0.79 us  [body(): pl.pallas_call(hand_over, out_shape=[jax.ShapeDtypeStruct(value.shape, f3...]
where the time goes in v2:
time: 23.8 us; the launch traced here: 23.7 us
  Pallas kernels  23.1 us (97%)
  between operations  0.64 us (3%)
    pallas_call x1, Pallas kernels, body(): pl.pallas_call(functools.partial(kernel, sizes), out_shape=(pltpu.VMEM((b...  22.3 us
    pallas_call x1, Pallas kernels, body(): pl.pallas_call(hand_over, out_shape=[jax.ShapeDtypeStruct(value.shape, f3...  0.79 us

profile of v2, /device:TPU:0, one launch (start us, length us, event | category | flops | bytes accessed | tf_op | source)
XLA Modules:
  0.0 23.7 jit_solution(8539802153380722614)
XLA Ops:
  0.6 22.3 %powers.1 = (f32[6,6,3,8,128]{4,3,2,1,0:T(8,128)S(1)}, f32[6,30]{1,0:T(8,128)S(1)}, f32[6,6]{1,0:T(8,128)S(1)}) custom-call(bf16[7,6,6,3,8,128]{5,4,3,2,1,0:T(8,128)(2,1)} %bitcast.6, f32[30,6,3,8,128]{4,3,2,1,0:T(8,128)} %bitcast.5, f32[6,3,8,128]{3,2,1,0:T(8,128)} %bitcast.7, f32[5]{0:T(128)} %shifts_hbm.1), custom_call_target="tpu_custom_call" | custom-call | tf_op jit(solution)/shard_map/powers/pallas_call | solution.py:841
  22.9 0.8 %hand_over.1 = (f32[6,6,3,8,128]{4,3,2,1,0:T(8,128)}, f32[6,30]{1,0:T(8,128)}, f32[6,6]{1,0:T(8,128)}) custom-call(f32[6,6,3,8,128]{4,3,2,1,0:T(8,128)S(1)} %get-tuple-element.9.new_in, f32[6,30]{1,0:T(8,128)S(1)} %get-tuple-element.10.proj_in, f32[6,6]{1,0:T(8,128)S(1)} %get-tuple-element.11.tri_in), custom_call_target="tpu_custom_call" | custom-call | tf_op jit(solution)/shard_map/hand_over/pallas_call | solution.py:902

commit v3 on v2

--- a/solution.py
+++ b/solution.py
@@ -128,7 +128,7 @@
     sizes, coef_hbm, early_hbm, start_hbm, shifts_hbm, new_ref, proj_ref, tri_ref,
     coef_in, coef, edge_coef, gx_in, gz_send, gz_in, gz, allv, pieces, part, acc_ref,
     halo_x, halo_z, send_z, send_c, halo_c, pre_x, pre_z, ghost_x, ghost_z,
-    ee, ee_cross, sums_ref, late_ref, small_ref,
+    ee, ee_cross, sums_ref, late_ref, small_ref, change_ref,
     mine_ee, gathered_ee, mine_b, gathered_b, mine_f, gathered_f,
     in_sem, face_send, face_recv, corner_send, corner_recv, g_send, g_recv,
     ee_send, ee_recv, b_send, b_recv, f_send, f_recv, ready, shifts_ref,
@@ -148,13 +148,19 @@
     lines = late // 2 + late % 2
 
     copy_start = pltpu.make_async_copy(start_hbm, allv.at[earlier], in_sem.at[0])
-    copy_coef = pltpu.make_async_copy(coef_hbm, coef_in, in_sem.at[1])
+    def coef_part(low, high, sem):
+        part = pl.ds(low, high - low)
+        return pltpu.make_async_copy(coef_hbm.at[part], coef_in.at[part], in_sem.at[sem])
+
+    kinds = coef_hbm.shape[0]
+    copy_height, copy_rest = coef_part(1, 3, 1), [coef_part(3, kinds, 4), coef_part(0, 1, 5)]
     copy_early = pltpu.make_async_copy(early_hbm, allv.at[pl.ds(0, earlier)], in_sem.at[2])
     copy_shifts = pltpu.make_async_copy(shifts_hbm, shifts_ref, in_sem.at[3])
     copy_start.start()
     copy_shifts.start()
-    copy_coef.start()
-    copy_early.start()
+    copy_height.start()
+    for copy in copy_rest:
+        copy.start()
 
     def there(kind, side, sending):
         upward = (side == 0) == sending
@@ -321,7 +327,7 @@
         )
 
     def apply_local(step):
-        acc = (1.0 - shifts_ref[step]) * allv[earlier + step]
+        acc = 0.0
         for e in range(comp):
             v = allv[earlier + step, e]
             near = [
@@ -416,7 +422,8 @@
         packed = whole[:ROWS]
         for g in range(1, 4):
             packed = packed + pltpu.roll(whole[ROWS * g:ROWS * (g + 1)], 32 * g, 1)
-        mine_ee[0] = packed
+        mine_ee[0, :ROWS] = packed
+        mine_ee[0, ROWS:] = as_line(sums_ref[0])
 
     exchanges = {
         "ee": (single, mine_ee, gathered_ee, ee_send, ee_recv),
@@ -465,10 +472,10 @@
             finish(name, at)
         return exchanges[name][1][len(stages)] * (1.0 / count)
 
-    def load_coefficients():
+    def load_height():
         @pl.loop(0, comp)
         def _(c):
-            for d in range(coef.shape[0]):
+            for d in (1, 2):
                 coef[d, c] = coef_in[d, c].astype(jnp.float32)
             for e in range(comp):
                 for x in range(width):
@@ -489,6 +496,12 @@
                 gz_send[side, ROWS * low:ROWS * (low + 2), :] = jnp.concatenate(
                     both, axis=0
                 ).astype(jnp.bfloat16)
+
+    def load_rest():
+        @pl.loop(0, comp)
+        def _(c):
+            for d in (0, *range(3, coef.shape[0])):
+                coef[d, c] = coef_in[d, c].astype(jnp.float32)
 
     def take_couplings():
         each_face(False, (0, 1), lambda kind, side: g_copy(kind, side).wait_recv())
@@ -546,6 +559,7 @@
 
     with jax.named_scope("start"):
         copy_start.wait()
+        copy_early.start()
         wait_around(barrier, REACH, (1, 1))
         greet(0)
 
@@ -572,17 +586,13 @@
             send_faces(r, step)
         if r == 0:
             with jax.named_scope("load"):
-                copy_coef.wait()
-                load_coefficients()
-                each_face(True, (0, 1), lambda kind, side: g_copy(kind, side).start())
-                copy_shifts.wait()
-        with jax.named_scope(f"neigh{r}"):
-            if size == 2 and r == paired[0]:
-                take_couplings()
-            if size == 2:
-                if r > paired[0]:
-                    each_corner(True, lambda sz, sx: corner_copy(r - 1, sz, sx).wait_send())
-                complete_neighbours(r, step)
+                copy_height.wait()
+                load_height()
+                each_face(True, (0,), lambda kind, side: g_copy(kind, side).start())
+                for copy in copy_rest:
+                    copy.wait()
+                each_face(True, (1,), lambda kind, side: g_copy(kind, side).start())
+                load_rest()
         with jax.named_scope(f"local{r}"):
             part[r] = apply_local(step)
         with jax.named_scope(f"part{r}"):
@@ -594,16 +604,26 @@
                         lambda kind, side: face_copy(r - 1, 0, 1, kind, side).wait_send(),
                     )
                 each_face(True, (0, 1), lambda kind, side: face_copy(r, step, 1, kind, side).start())
-            if r == 0:
+        with jax.named_scope(f"neigh{r}"):
+            if size == 2 and r == paired[0]:
+                take_couplings()
+            if size == 2:
+                if r > paired[0]:
+                    each_corner(True, lambda sz, sx: corner_copy(r - 1, sz, sx).wait_send())
+                complete_neighbours(r, step)
+        with jax.named_scope(f"cross{r}"):
+            if len(rounds) == 1:
                 copy_early.wait()
-        with jax.named_scope(f"cross{r}"):
-            for k in range(done, min(step + 1, late)):
-                cross_products(k, sums_ref.at[k // 2], (k % 2) * half)
-                done = k + 1
+            if r or len(rounds) == 1:
+                for k in range(done, min(step + 1, late)):
+                    cross_products(k, sums_ref.at[k // 2], (k % 2) * half)
+                    done = k + 1
         with jax.named_scope(f"self{r}"):
             if share[r]:
                 middle = self_at + share[r] // 2
                 if r == 0:
+                    if len(rounds) > 1:
+                        copy_early.wait()
                     self_some(self_at, middle)
                     greet(greeted)
                     greeted += 1
@@ -615,6 +635,10 @@
                     self_some(self_at, self_at + share[r])
                 self_at += share[r]
         with jax.named_scope(f"ee{r}"):
+            if done == late and r == len(rounds) - 1:
+                for q in range(1, lines):
+                    mine_b[0, q - 1] = as_line(sums_ref[q])
+                begin("b", 0)
             if share[r] and self_at == comp:
                 self_finish()
                 while greeted <= levels:
@@ -626,10 +650,6 @@
                 finish("ee", 0)
                 begin("ee", 1)
                 ee_at = 1
-            if done == late and r == len(rounds) - 1:
-                for q in range(lines):
-                    mine_b[0, q] = as_line(sums_ref[q])
-                begin("b", 0)
         with jax.named_scope(f"faces{r}"):
             take_faces(r, step, lambda x, r=r: part[r, :, x])
         if size == 2:
@@ -656,15 +676,35 @@
             if at > ee_at:
                 begin("ee", at)
             finish("ee", at)
-        packed = mine_ee[len(single)] * (1.0 / count)
+        packed = mine_ee[len(single), :ROWS] * (1.0 / count)
+        ahead = mine_ee[len(single), ROWS:] * (1.0 / count)
+    row, lane = iota((ROWS, LANES), 0), iota((ROWS, LANES), 1)
+    with jax.named_scope("change"):
+        copy_shifts.wait()
+        unit, nothing = jnp.ones((ROWS, LANES), jnp.float32), jnp.zeros((ROWS, LANES), jnp.float32)
+        change = [[unit]]
+        for k in range(depth):
+            last, scale = change[-1], 1.0 - shifts_ref[k]
+            change.append(
+                [
+                    (last[m - 1] if m else nothing) + (scale * last[m] if m <= k else nothing)
+                    for m in range(k + 2)
+                ]
+            )
+        for m in range(block):
+            down, along = nothing, nothing
+            for k in range(m, block):
+                down = jnp.where(row == k, change[k][m], down)
+                along = jnp.where(lane == k, change[k][m], along)
+            change_ref[0, m] = down
+            change_ref[1, m] = along
     with jax.named_scope("bwait"):
         early = whole_exchange("b", True)
 
     with jax.named_scope("algebra"):
-        row, lane = iota((ROWS, LANES), 0), iota((ROWS, LANES), 1)
         found = jnp.concatenate(
             [
-                early[k // 2] if k % 2 == 0 else pltpu.roll(early[k // 2], half, 1)
+                pltpu.roll(ahead if k < 2 else early[k // 2 - 1], (k % 2) * half, 1)
                 for k in range(late)
             ] + [jnp.zeros((ROWS - late, LANES), jnp.float32)], axis=0
         )
@@ -696,9 +736,19 @@
         onto = dot(inverse, moved)
 
         mix = dot(inverse, pick - proj_t)
-        tall = dot(onehot((late * ROWS, ROWS), lambda r, q: (r >> 3) == q), mix)
+        tall = jnp.concatenate(
+            [jnp.broadcast_to(mix[k:k + 1], (ROWS, LANES)) for k in range(late)], axis=0
+        )
         span = earlier * ROWS
-        mix = split(diagonal(dot(tall, onehot((LANES, span), lambda r, q: (q >> 3) == r))))
+        grow = onehot((LANES, span), lambda r, q: (q >> 3) == r).astype(jnp.bfloat16)
+        mix = [
+            diagonal(
+                lax.dot_general(
+                    piece, grow, (((1,), (0,)), ((), ())), preferred_element_type=jnp.float32
+                )
+            ).astype(jnp.bfloat16)
+            for piece in split(tall)
+        ]
         weights = [
             [
                 jnp.broadcast_to(
@@ -717,9 +767,13 @@
                     for i in range(k + 1):
                         value = value + weights[k][i] * allv[earlier + i, c, x]
                     new_ref[k, c, x] = value
-        small_ref[0:ROWS, :] = proj_t
-        small_ref[ROWS:2 * ROWS, :] = jnp.zeros((ROWS, LANES), jnp.float32)
-        small_ref[ROWS:2 * ROWS, 0:ROWS] = jnp.where((q8 >= r8) & (r8 < late), upper, 0.0)
+        proj_early, tri_early = 0.0, 0.0
+        for m in range(late):
+            proj_early = proj_early + change_ref[0, m] * proj_t[m:m + 1]
+            column = jnp.where(r8[:, :1] <= m, upper[:, m:m + 1], 0.0)
+            tri_early = tri_early + change_ref[1, m] * column
+        small_ref[0:ROWS, :] = proj_early
+        small_ref[ROWS:2 * ROWS, :] = jnp.where(row < late, tri_early, 0.0)
 
     with jax.named_scope("sent"):
         r = len(rounds) - 1
@@ -772,11 +826,11 @@
         triangle = small_ref[ROWS:2 * ROWS, :]
         proj_rows = small_ref[0:ROWS, :]
         for b in range(fresh):
-            k = late + b
-            triangle = triangle + jnp.where(lane == k, wide(columns[b][2]), 0.0)
+            column = wide(columns[b][2])
             for a in range(b + 1):
-                triangle = triangle + jnp.where((lane == k) & (row == late + a), ratios[a, b], 0.0)
-            proj_rows = jnp.where((row == k) & (lane < earlier), spread[b], proj_rows)
+                column = jnp.where(row == late + a, ratios[a, b], column)
+            triangle = triangle + change_ref[1, late + b] * column
+            proj_rows = proj_rows + change_ref[0, late + b] * spread[b]
         small_ref[ROWS:2 * ROWS, :] = triangle
         small_ref[0:ROWS, :] = proj_rows
         for b in range(fresh):
@@ -873,13 +927,14 @@
             pltpu.VMEM((lines, lanes, lanes), f32),
             pltpu.VMEM((lanes, lanes), f32),
             pltpu.VMEM((2 * rows, lanes), f32),
-            pltpu.VMEM((len(single) + 1, rows, lanes), f32),
-            pltpu.VMEM((len(single), most, rows, lanes), f32),
-            pltpu.VMEM((len(joint) + 1, lines, 1, lanes), f32),
-            pltpu.VMEM((len(joint), joined, lines, 1, lanes), f32),
+            pltpu.VMEM((2, block, rows, lanes), f32),
+            pltpu.VMEM((len(single) + 1, rows + 1, lanes), f32),
+            pltpu.VMEM((len(single), most, rows + 1, lanes), f32),
+            pltpu.VMEM((len(joint) + 1, max(1, lines - 1), 1, lanes), f32),
+            pltpu.VMEM((len(joint), joined, max(1, lines - 1), 1, lanes), f32),
             pltpu.VMEM((len(joint) + 1, 1, lanes), f32),
             pltpu.VMEM((len(joint), joined, 1, lanes), f32),
-            sems((4,)),
+            sems((6,)),
             sems((2, 2, 2)),
             sems((2, 2, 2, 2)),
             sems((2, 2)),

time: 23.8 us -> 23.2 us (0.975)
  Pallas kernels: 23.1 us -> 22.4 us
    pallas_call x1, Pallas kernels: 22.3 us -> 21.6 us  [body(): pl.pallas_call(functools.partial(kernel, sizes), out_shape=(pltpu.VMEM((b...]
where the time goes in v3:
time: 23.2 us; the launch traced here: 23 us
  Pallas kernels  22.4 us (97%)
  between operations  0.64 us (3%)
    pallas_call x1, Pallas kernels, body(): pl.pallas_call(functools.partial(kernel, sizes), out_shape=(pltpu.VMEM((b...  21.6 us
    pallas_call x1, Pallas kernels, body(): pl.pallas_call(hand_over, out_shape=[jax.ShapeDtypeStruct(value.shape, f3...  0.79 us

profile of v3, /device:TPU:0, one launch (start us, length us, event | category | flops | bytes accessed | tf_op | source)
XLA Modules:
  0.0 23.0 jit_solution(7420045275571774861)
XLA Ops:
  0.6 21.6 %powers.1 = (f32[6,6,3,8,128]{4,3,2,1,0:T(8,128)S(1)}, f32[6,30]{1,0:T(8,128)S(1)}, f32[6,6]{1,0:T(8,128)S(1)}) custom-call(bf16[7,6,6,3,8,128]{5,4,3,2,1,0:T(8,128)(2,1)} %bitcast.6, f32[30,6,3,8,128]{4,3,2,1,0:T(8,128)} %bitcast.5, f32[6,3,8,128]{3,2,1,0:T(8,128)} %bitcast.7, f32[5]{0:T(128)} %shifts_hbm.1), custom_call_target="tpu_custom_call" | custom-call | tf_op jit(solution)/shard_map/powers/pallas_call | solution.py:895
  22.2 0.8 %hand_over.1 = (f32[6,6,3,8,128]{4,3,2,1,0:T(8,128)}, f32[6,30]{1,0:T(8,128)}, f32[6,6]{1,0:T(8,128)}) custom-call(f32[6,6,3,8,128]{4,3,2,1,0:T(8,128)S(1)} %get-tuple-element.9.new_in, f32[6,30]{1,0:T(8,128)S(1)} %get-tuple-element.10.proj_in, f32[6,6]{1,0:T(8,128)S(1)} %get-tuple-element.11.tri_in), custom_call_target="tpu_custom_call" | custom-call | tf_op jit(solution)/shard_map/hand_over/pallas_call | solution.py:957

commit v4 on v3

--- a/solution.py
+++ b/solution.py
@@ -128,9 +128,9 @@
     sizes, coef_hbm, early_hbm, start_hbm, shifts_hbm, new_ref, proj_ref, tri_ref,
     coef_in, coef, edge_coef, gx_in, gz_send, gz_in, gz, allv, pieces, part, acc_ref,
     halo_x, halo_z, send_z, send_c, halo_c, pre_x, pre_z, ghost_x, ghost_z,
-    ee, ee_cross, sums_ref, late_ref, small_ref, change_ref,
+    edge_ref, ee, ee_cross, sums_ref, late_ref, small_ref, change_ref,
     mine_ee, gathered_ee, mine_b, gathered_b, mine_f, gathered_f,
-    in_sem, face_send, face_recv, corner_send, corner_recv, g_send, g_recv,
+    in_sem, face_send, face_recv, corner_send, corner_recv, g_recv,
     ee_send, ee_recv, b_send, b_recv, f_send, f_recv, ready, shifts_ref,
 ):
     depth = shifts_ref.shape[0]
@@ -139,6 +139,7 @@
     count = comp * width * ROWS * LANES * sizes[0][1] * sizes[1][1]
     half = LANES // 2
     rounds = steps_of(depth)
+    paired = [r for r, size in enumerate(rounds) if size == 2]
     single = stages_of(sizes)[::-1]
     joint = joint_stages_of(sizes)
     place = [lax.axis_index(axis) for axis, _ in sizes]
@@ -240,8 +241,7 @@
                 for r in range(len(rounds)):
                     halo_c[r, sz, sx] = jnp.zeros_like(halo_c[r, sz, sx])
 
-    send_z[...] = jnp.zeros_like(send_z)
-    send_c[...] = jnp.zeros_like(send_c)
+    edge_ref[...] = jnp.zeros_like(edge_ref)
     edge_coef[...] = jnp.zeros_like(edge_coef)
     ee[...] = jnp.zeros_like(ee)
     ee_cross[...] = jnp.zeros_like(ee_cross)
@@ -258,15 +258,14 @@
         dz, dx = (toward(side), 0) if kind == 0 else (0, toward(side))
         return pltpu.make_async_remote_copy(
             src_ref=src, dst_ref=dst,
-            send_sem=face_send.at[what, kind, side],
-            recv_sem=face_recv.at[r % 2, what, kind, side],
+            send_sem=face_send.at[what, kind], recv_sem=face_recv.at[r % 2, what, kind],
             device_id=at_peer(dz, dx), device_id_type=MESH,
         )
 
     def corner_copy(r, sz, sx):
         return pltpu.make_async_remote_copy(
             src_ref=send_c.at[r, sz, sx], dst_ref=halo_c.at[r, sz, sx],
-            send_sem=corner_send.at[sz, sx], recv_sem=corner_recv.at[r % 2, sz, sx],
+            send_sem=corner_send.at[0], recv_sem=corner_recv.at[r % 2],
             device_id=at_peer(toward(sz), toward(sx)), device_id_type=MESH,
         )
 
@@ -278,8 +277,8 @@
             dst = gx_in.at[side]
         dz, dx = (toward(side), 0) if kind == 0 else (0, toward(side))
         return pltpu.make_async_remote_copy(
-            src_ref=src, dst_ref=dst, send_sem=g_send.at[kind, side],
-            recv_sem=g_recv.at[kind, side], device_id=at_peer(dz, dx), device_id_type=MESH,
+            src_ref=src, dst_ref=dst, send_sem=face_send.at[1, kind],
+            recv_sem=g_recv.at[kind], device_id=at_peer(dz, dx), device_id_type=MESH,
         )
 
     def each_face(sending, kinds, act):
@@ -296,10 +295,45 @@
                 def _():
                     act(sz, sx)
 
+    def amount(ref, send_sem, recv_sem, sending):
+        copy = pltpu.make_async_remote_copy(
+            src_ref=ref, dst_ref=ref, send_sem=send_sem, recv_sem=recv_sem,
+            device_id=at_peer(0, 0), device_id_type=MESH,
+        )
+        return copy.wait_send if sending else copy.wait_recv
+
+    def both(kind, sending):
+        return there(kind, 0, sending) & there(kind, 1, sending)
+
+    def single_side(kind, sending):
+        return there(kind, 0, sending) ^ there(kind, 1, sending)
+
+    def wait_faces(r, what, kinds, sending):
+        for kind in kinds:
+            halo = (halo_z, halo_x)[kind]
+            sems = (face_send.at[what, kind], face_recv.at[r % 2, what, kind], sending)
+            pl.when(both(kind, sending))(lambda: amount(halo.at[r, what], *sems)())
+            pl.when(single_side(kind, sending))(lambda: amount(halo.at[r, what, 0], *sems)())
+
+    def wait_corners(r, sending):
+        sems = (corner_send.at[0], corner_recv.at[r % 2], sending)
+        two = [both(kind, sending) for kind in (0, 1)]
+        one = [single_side(kind, sending) for kind in (0, 1)]
+        pl.when(two[0] & two[1])(lambda: amount(halo_c.at[r], *sems)())
+        pl.when((two[0] & one[1]) | (one[0] & two[1]))(lambda: amount(halo_c.at[r, 0], *sems)())
+        pl.when(one[0] & one[1])(lambda: amount(halo_c.at[r, 0, 0], *sems)())
+
+    def wait_couplings(sending):
+        for kind in (0, 1):
+            held = (gz_in, gx_in)[kind]
+            sems = (face_send.at[1, kind], g_recv.at[kind], sending)
+            pl.when(both(kind, sending))(lambda: amount(held, *sems)())
+            pl.when(single_side(kind, sending))(lambda: amount(held.at[0], *sems)())
+
     def pack(r, what, source):
         for e in range(comp):
             for x in range(width):
-                row = 4 * e + x
+                row = width * e + x
                 tile = source(e, x)
                 send_z[r, what, 0, row:row + 1, :] = tile[ROWS - 1:ROWS, :]
                 send_z[r, what, 1, row:row + 1, :] = tile[0:1, :]
@@ -319,12 +353,12 @@
             return jnp.where(low_rows, pltpu.roll(below, 4, 0), above)
         return jnp.where(low_rows, below, pltpu.roll(above, 4, 0))
 
-    def pair_tile(ref, index, e):
-        base = ROWS * (e // 2)
-        return split_pair(
-            ref[(*index, 0, slice(base, base + ROWS))],
-            ref[(*index, 1, slice(base, base + ROWS))], e % 2,
-        )
+    def spread_edges(below, above):
+        for e in range(comp):
+            for x in range(width):
+                at = width * e + x
+                edge_ref[e, x:x + 1, :] = below[at:at + 1, :]
+                edge_ref[e, 4 + x:5 + x, :] = above[at:at + 1, :]
 
     def apply_local(step):
         acc = 0.0
@@ -369,10 +403,11 @@
                 allv[earlier + step, c, x] = value
 
     def take_faces(r, step, source):
-        each_face(False, (1,), lambda kind, side: face_copy(r, step, 0, kind, side).wait_recv())
+        wait_faces(r, 0, (1,), False)
         sides = add_x(source, lambda side, e: halo_x[r, 0, side, e])
-        each_face(False, (0,), lambda kind, side: face_copy(r, step, 0, kind, side).wait_recv())
-        edge = add_z(lambda e: pair_tile(halo_z, (r, 0), e))
+        wait_faces(r, 0, (0,), False)
+        spread_edges(halo_z.at[r, 0, 0], halo_z.at[r, 0, 1])
+        edge = add_z(lambda e: edge_ref[e])
         store_step(step + 1, source, sides, edge)
 
     def cross_products(k, ref, base):
@@ -504,7 +539,7 @@
                 coef[d, c] = coef_in[d, c].astype(jnp.float32)
 
     def take_couplings():
-        each_face(False, (0, 1), lambda kind, side: g_copy(kind, side).wait_recv())
+        wait_couplings(False)
         for low in range(0, comp * comp // 2, 2):
             below = gz_in[0, ROWS * low:ROWS * (low + 2), :].astype(jnp.float32)
             above = gz_in[1, ROWS * low:ROWS * (low + 2), :].astype(jnp.float32)
@@ -522,12 +557,9 @@
                     value = value + gx_in[side, c, e].astype(jnp.float32) * allv[earlier + step, e, x]
                 pre_x[side, c] = value
         total = jnp.zeros((comp, ROWS, LANES), jnp.float32)
+        spread_edges(send_z.at[r, 0, 1], send_z.at[r, 0, 0])
         for e in range(comp):
-            base = ROWS * (e // 2)
-            own = split_pair(
-                send_z[r, 0, 1, base:base + ROWS, :], send_z[r, 0, 0, base:base + ROWS, :], e % 2
-            )
-            total = total + gz[:, e] * own[None]
+            total = total + gz[:, e] * edge_ref[e][None]
         pre_z[...] = total
         for sz in (0, 1):
             for sx in (0, 1):
@@ -535,14 +567,15 @@
                 x = (4 if sz == 0 else 0) + (width - 1 if sx == 0 else 0)
                 for c in range(comp):
                     send_c[r, sz, sx, c:c + 1, :] = pre_x[1 - sx, c, z:z + 1, :]
-                    send_c[r, sz, sx, ROWS + c:ROWS + c + 1, :] = pre_z[c, x:x + 1, :]
+                    send_c[r, sz, sx, comp + c:comp + c + 1, :] = pre_z[c, x:x + 1, :]
         each_corner(True, lambda sz, sx: corner_copy(r, sz, sx).start())
 
     def take_ghosts(r, step):
-        each_face(False, (1, 0), lambda kind, side: face_copy(r, step, 1, kind, side).wait_recv())
-        each_corner(False, lambda sz, sx: corner_copy(r, sz, sx).wait_recv())
+        wait_faces(r, 1, (1, 0), False)
+        wait_corners(r, False)
+        spread_edges(halo_z.at[r, 1, 0], halo_z.at[r, 1, 1])
         for c in range(comp):
-            value = pair_tile(halo_z, (r, 1), c) + pre_z[c]
+            value = edge_ref[c] + pre_z[c]
             for sz in (0, 1):
                 for sx in (0, 1):
                     row = (0 if sz == 0 else 4) + (0 if sx == 0 else width - 1)
@@ -553,7 +586,7 @@
                 for sz in (0, 1):
                     row = 0 if sz == 0 else ROWS - 1
                     value = value + jnp.where(
-                        row2 == row, halo_c[r, sz, side, ROWS + c:ROWS + c + 1, :], 0.0
+                        row2 == row, halo_c[r, sz, side, comp + c:comp + c + 1, :], 0.0
                     )
                 ghost_x[side, c] = value
 
@@ -565,7 +598,6 @@
 
     step = 0
     comps = list(range(comp))
-    paired = [r for r, size in enumerate(rounds) if size == 2]
     before = max(1, len(rounds) - 1)
     share = [2 * comp // (before + 1)] + [comp // (before + 1)] * (before - 1)
     share[-1] += comp - sum(share)
@@ -580,18 +612,16 @@
     for r, size in enumerate(rounds):
         with jax.named_scope(f"send{r}"):
             if r:
-                each_face(
-                    True, (0, 1), lambda kind, side: face_copy(r - 1, 0, 0, kind, side).wait_send()
-                )
+                wait_faces(r - 1, 0, (0, 1), True)
             send_faces(r, step)
         if r == 0:
             with jax.named_scope("load"):
                 copy_height.wait()
                 load_height()
-                each_face(True, (0,), lambda kind, side: g_copy(kind, side).start())
+                each_face(True, (0,) if paired else (), lambda kind, side: g_copy(kind, side).start())
                 for copy in copy_rest:
                     copy.wait()
-                each_face(True, (1,), lambda kind, side: g_copy(kind, side).start())
+                each_face(True, (1,) if paired else (), lambda kind, side: g_copy(kind, side).start())
                 load_rest()
         with jax.named_scope(f"local{r}"):
             part[r] = apply_local(step)
@@ -599,17 +629,16 @@
             if size == 2:
                 pack(r, 1, lambda e, x: part.at[r, e, x])
                 if r > paired[0]:
-                    each_face(
-                        True, (0, 1),
-                        lambda kind, side: face_copy(r - 1, 0, 1, kind, side).wait_send(),
-                    )
+                    wait_faces(r - 1, 1, (0, 1), True)
+                else:
+                    wait_couplings(True)
                 each_face(True, (0, 1), lambda kind, side: face_copy(r, step, 1, kind, side).start())
         with jax.named_scope(f"neigh{r}"):
             if size == 2 and r == paired[0]:
                 take_couplings()
             if size == 2:
                 if r > paired[0]:
-                    each_corner(True, lambda sz, sx: corner_copy(r - 1, sz, sx).wait_send())
+                    wait_corners(r - 1, True)
                 complete_neighbours(r, step)
         with jax.named_scope(f"cross{r}"):
             if len(rounds) == 1:
@@ -776,15 +805,10 @@
         small_ref[ROWS:2 * ROWS, :] = jnp.where(row < late, tri_early, 0.0)
 
     with jax.named_scope("sent"):
-        r = len(rounds) - 1
-        for what in range(2 if paired else 1):
-            at = paired[-1] if what else r
-            each_face(
-                True, (0, 1), lambda kind, side: face_copy(at, 0, what, kind, side).wait_send()
-            )
+        wait_faces(len(rounds) - 1, 0, (0, 1), True)
         if paired:
-            each_corner(True, lambda sz, sx: corner_copy(paired[-1], sz, sx).wait_send())
-        each_face(True, (0, 1), lambda kind, side: g_copy(kind, side).wait_send())
+            wait_faces(paired[-1], 1, (0, 1), True)
+            wait_corners(paired[-1], True)
         drain("ee")
         drain("b")
     with jax.named_scope("fwait"):
@@ -914,13 +938,14 @@
             pltpu.VMEM((rounds, comp, width, rows, lanes), f32),
             pltpu.VMEM((comp, width, rows, lanes), f32),
             pltpu.VMEM((rounds, 2, 2, comp, rows, lanes), f32),
-            pltpu.VMEM((rounds, 2, 2, 4 * comp, lanes), f32),
-            pltpu.VMEM((rounds, 2, 2, 4 * comp, lanes), f32),
-            pltpu.VMEM((rounds, 2, 2, 2 * rows, lanes), f32),
-            pltpu.VMEM((rounds, 2, 2, 2 * rows, lanes), f32),
+            pltpu.VMEM((rounds, 2, 2, width * comp, lanes), f32),
+            pltpu.VMEM((rounds, 2, 2, width * comp, lanes), f32),
+            pltpu.VMEM((rounds, 2, 2, 2 * comp, lanes), f32),
+            pltpu.VMEM((rounds, 2, 2, 2 * comp, lanes), f32),
             pltpu.VMEM((2, comp, rows, lanes), f32),
             pltpu.VMEM((comp, rows, lanes), f32),
             pltpu.VMEM((2, comp, rows, lanes), f32),
+            pltpu.VMEM((comp, rows, lanes), f32),
             pltpu.VMEM((comp, rows, lanes), f32),
             pltpu.VMEM((count * rows, count * rows), f32),
             pltpu.VMEM((count * rows, count * rows), f32),
@@ -935,12 +960,11 @@
             pltpu.VMEM((len(joint) + 1, 1, lanes), f32),
             pltpu.VMEM((len(joint), joined, 1, lanes), f32),
             sems((6,)),
-            sems((2, 2, 2)),
-            sems((2, 2, 2, 2)),
             sems((2, 2)),
             sems((2, 2, 2)),
-            sems((2, 2)),
-            sems((2, 2)),
+            sems((1,)),
+            sems((2,)),
+            sems((2,)),
             sems((len(single),)),
             sems((len(single),)),
             sems((len(joint),)),

time: 23.2 us -> 22.7 us (0.978)
  Pallas kernels: 22.4 us -> 21.9 us
    pallas_call x1, Pallas kernels: 21.6 us -> 21.1 us  [body(): pl.pallas_call(functools.partial(kernel, sizes), out_shape=(pltpu.VMEM((b...]
where the time goes in v4:
time: 22.7 us; the launch traced here: 22.5 us
  Pallas kernels  21.9 us (96%)
  between operations  0.64 us (3%)
    pallas_call x1, Pallas kernels, body(): pl.pallas_call(functools.partial(kernel, sizes), out_shape=(pltpu.VMEM((b...  21.1 us
    pallas_call x1, Pallas kernels, body(): pl.pallas_call(hand_over, out_shape=[jax.ShapeDtypeStruct(value.shape, f3...  0.79 us

profile of v4, /device:TPU:0, one launch (start us, length us, event | category | flops | bytes accessed | tf_op | source)
XLA Modules:
  0.0 22.5 jit_solution(14294929971765350437)
XLA Ops:
  0.6 21.1 %powers.1 = (f32[6,6,3,8,128]{4,3,2,1,0:T(8,128)S(1)}, f32[6,30]{1,0:T(8,128)S(1)}, f32[6,6]{1,0:T(8,128)S(1)}) custom-call(bf16[7,6,6,3,8,128]{5,4,3,2,1,0:T(8,128)(2,1)} %bitcast.6, f32[30,6,3,8,128]{4,3,2,1,0:T(8,128)} %bitcast.5, f32[6,3,8,128]{3,2,1,0:T(8,128)} %bitcast.7, f32[5]{0:T(128)} %shifts_hbm.1), custom_call_target="tpu_custom_call" | custom-call | tf_op jit(solution)/shard_map/powers/pallas_call | solution.py:919
  21.7 0.8 %hand_over.1 = (f32[6,6,3,8,128]{4,3,2,1,0:T(8,128)}, f32[6,30]{1,0:T(8,128)}, f32[6,6]{1,0:T(8,128)}) custom-call(f32[6,6,3,8,128]{4,3,2,1,0:T(8,128)S(1)} %get-tuple-element.9.new_in, f32[6,30]{1,0:T(8,128)S(1)} %get-tuple-element.10.proj_in, f32[6,6]{1,0:T(8,128)S(1)} %get-tuple-element.11.tri_in), custom_call_target="tpu_custom_call" | custom-call | tf_op jit(solution)/shard_map/hand_over/pallas_call | solution.py:981

commit v5 on v4

--- a/solution.py
+++ b/solution.py
@@ -126,7 +126,7 @@
 
 def kernel(
     sizes, coef_hbm, early_hbm, start_hbm, shifts_hbm, new_ref, proj_ref, tri_ref,
-    coef_in, coef, edge_coef, gx_in, gz_send, gz_in, gz, allv, pieces, part, acc_ref,
+    coef_in, coef, edge_coef, gx_in, gz_send, gz_in, flat_ref, gz, allv, pieces, part, acc_ref,
     halo_x, halo_z, send_z, send_c, halo_c, pre_x, pre_z, ghost_x, ghost_z,
     edge_ref, ee, ee_cross, sums_ref, late_ref, small_ref, change_ref,
     mine_ee, gathered_ee, mine_b, gathered_b, mine_f, gathered_f,
@@ -242,6 +242,8 @@
                     halo_c[r, sz, sx] = jnp.zeros_like(halo_c[r, sz, sx])
 
     edge_ref[...] = jnp.zeros_like(edge_ref)
+    flat_ref[...] = jnp.zeros_like(flat_ref)
+    gz[...] = jnp.zeros_like(gz)
     edge_coef[...] = jnp.zeros_like(edge_coef)
     ee[...] = jnp.zeros_like(ee)
     ee_cross[...] = jnp.zeros_like(ee_cross)
@@ -346,12 +348,6 @@
     row3 = iota((width, ROWS, LANES), 1)
     lane3 = iota((width, ROWS, LANES), 2)
     zero_tile = jnp.zeros((1, ROWS, LANES), jnp.float32)
-    low_rows = row2 < 4
-
-    def split_pair(below, above, odd):
-        if odd:
-            return jnp.where(low_rows, pltpu.roll(below, 4, 0), above)
-        return jnp.where(low_rows, below, pltpu.roll(above, 4, 0))
 
     def spread_edges(below, above):
         for e in range(comp):
@@ -517,20 +513,11 @@
                     edge_coef[c, e, x:x + 1, :] = coef[1, c, e, x, 0:1, :]
                     edge_coef[c, e, 4 + x:5 + x, :] = coef[2, c, e, x, ROWS - 1:ROWS, :]
 
-        flat = comp * comp // 2
-        for low in range(0, flat, 2):
-            for side in (0, 1):
-                both = []
-                for at in (low, low + 1):
-                    c, e = 2 * at // comp, 2 * at % comp
-                    one, two = edge_coef[c, e], edge_coef[c, e + 1]
-                    if side == 0:
-                        both.append(jnp.where(low_rows, pltpu.roll(one, 4, 0), two))
-                    else:
-                        both.append(jnp.where(low_rows, one, pltpu.roll(two, 4, 0)))
-                gz_send[side, ROWS * low:ROWS * (low + 2), :] = jnp.concatenate(
-                    both, axis=0
-                ).astype(jnp.bfloat16)
+        for at in range(comp * comp * width):
+            c, e, x = at // (comp * width), at // width % comp, at % width
+            flat_ref[0, at:at + 1, :] = edge_coef[c, e, 4 + x:5 + x, :]
+            flat_ref[1, at:at + 1, :] = edge_coef[c, e, x:x + 1, :]
+        gz_send[...] = flat_ref[...].astype(jnp.bfloat16)
 
     def load_rest():
         @pl.loop(0, comp)
@@ -540,14 +527,11 @@
 
     def take_couplings():
         wait_couplings(False)
-        for low in range(0, comp * comp // 2, 2):
-            below = gz_in[0, ROWS * low:ROWS * (low + 2), :].astype(jnp.float32)
-            above = gz_in[1, ROWS * low:ROWS * (low + 2), :].astype(jnp.float32)
-            for at in (0, 1):
-                c, e = 2 * (low + at) // comp, 2 * (low + at) % comp
-                b, a = below[ROWS * at:ROWS * (at + 1)], above[ROWS * at:ROWS * (at + 1)]
-                gz[c, e] = split_pair(b, a, 0)
-                gz[c, e + 1] = split_pair(b, a, 1)
+        flat_ref[...] = gz_in[...].astype(jnp.float32)
+        for at in range(comp * comp * width):
+            c, e, x = at // (comp * width), at // width % comp, at % width
+            gz[c, e, x:x + 1, :] = flat_ref[0, at:at + 1, :]
+            gz[c, e, 4 + x:5 + x, :] = flat_ref[1, at:at + 1, :]
 
     def complete_neighbours(r, step):
         for side, x in ((0, 0), (1, width - 1)):
@@ -906,6 +890,7 @@
     block = depth + 1
     kinds, comp, _, width, rows, lanes = coefficients.shape
     rounds = len(steps_of(depth))
+    flat = -(-comp * comp * width // 16) * 16
     late = block - steps_of(depth)[-1]
     lines = late // 2 + late % 2
     single, joint = stages_of(sizes), joint_stages_of(sizes)
@@ -930,8 +915,9 @@
             pltpu.VMEM(coefficients.shape, f32),
             pltpu.VMEM((comp, comp, rows, lanes), f32),
             pltpu.VMEM((2, comp, comp, rows, lanes), b16),
-            pltpu.VMEM((2, 4 * comp * comp, lanes), b16),
-            pltpu.VMEM((2, 4 * comp * comp, lanes), b16),
+            pltpu.VMEM((2, flat, lanes), b16),
+            pltpu.VMEM((2, flat, lanes), b16),
+            pltpu.VMEM((2, flat, lanes), f32),
             pltpu.VMEM((comp, comp, rows, lanes), f32),
             pltpu.VMEM((count + block, comp, width, rows, lanes), f32),
             pltpu.VMEM((3, comp, count * rows, width * lanes), b16),

time: 22.7 us -> 22.5 us (level)
  no operation moved by 1% of the time
where the time goes in v5:
time: 22.5 us; the launch traced here: 22.4 us
  Pallas kernels  21.7 us (96%)
  between operations  0.64 us (3%)
    pallas_call x1, Pallas kernels, body(): pl.pallas_call(functools.partial(kernel, sizes), out_shape=(pltpu.VMEM((b...  20.9 us
    pallas_call x1, Pallas kernels, body(): pl.pallas_call(hand_over, out_shape=[jax.ShapeDtypeStruct(value.shape, f3...  0.79 us

profile of v5, /device:TPU:0, one launch (start us, length us, event | category | flops | bytes accessed | tf_op | source)
XLA Modules:
  0.0 22.4 jit_solution(13691302635148946805)
XLA Ops:
  0.6 20.9 %powers.1 = (f32[6,6,3,8,128]{4,3,2,1,0:T(8,128)S(1)}, f32[6,30]{1,0:T(8,128)S(1)}, f32[6,6]{1,0:T(8,128)S(1)}) custom-call(bf16[7,6,6,3,8,128]{5,4,3,2,1,0:T(8,128)(2,1)} %bitcast.6, f32[30,6,3,8,128]{4,3,2,1,0:T(8,128)} %bitcast.5, f32[6,3,8,128]{3,2,1,0:T(8,128)} %bitcast.7, f32[5]{0:T(128)} %shifts_hbm.1), custom_call_target="tpu_custom_call" | custom-call | tf_op jit(solution)/shard_map/powers/pallas_call | solution.py:904
  21.6 0.8 %hand_over.1 = (f32[6,6,3,8,128]{4,3,2,1,0:T(8,128)}, f32[6,30]{1,0:T(8,128)}, f32[6,6]{1,0:T(8,128)}) custom-call(f32[6,6,3,8,128]{4,3,2,1,0:T(8,128)S(1)} %get-tuple-element.9.new_in, f32[6,30]{1,0:T(8,128)S(1)} %get-tuple-element.10.proj_in, f32[6,6]{1,0:T(8,128)S(1)} %get-tuple-element.11.tri_in), custom_call_target="tpu_custom_call" | custom-call | tf_op jit(solution)/shard_map/hand_over/pallas_call | solution.py:967
